TPU v7x, 256 devices: a 2x2x32 block of a 4x8x32 slice. The times are simulated.
256 devices in a mesh: groups: 4 (over y, x), expert: 64 (over z, core).
Axes of the slice: x: 2, y: 2, z: 32, core: 2. Of those that a mesh axis runs over, the one named last changes fastest.
The devices are a block of a 4x8x32 slice.
Arguments:
- tokens: bfloat16 [32768, 4096], P(('groups', 'expert')), parts along dimension 0, may hold values from -6 to 6
- router_weight: bfloat16 [4096, 128], replicated, may hold values from -0.078125 to 0.078125
- expert_ids: int32 [32768, 8], P(('groups', 'expert')), parts along dimension 0, may hold values from 0 to 127, all different within a row; in each aligned block of 128 rows (0 to 127, 128 to 255, ...) at most 9 rows name the same one
Outputs:
- expert_rows: bfloat16 [128, 2304, 4096], P('expert', 'groups'), parts along dimension 1
- balance_loss: float32 [4], P('groups'), parts along dimension 0
There are 4 independent parts, one for each index of `groups`. A program takes and returns all parts, laid end to end along the dimension named above; an argument that names none is the same for every part. Nothing has to cross between parts.
Inputs may be any that keep to these rules, and one draw needn't show every extreme that they name: `expert_ids`: each row names 8 different experts; among the rows of one device no expert is named more than 9 times, a bound that some block reaches.
All inputs are finite; a program needn't handle non-finite values.
Results may differ from a plain program's by a relative error of at most 0.0012.
Values may be sent and summed in bfloat16 or wider, within the bound.
No kernel may reach another device: no remote copies, remote signals or barrier semaphores. Data moves between devices by JAX's collectives and lax.ppermute only.
A program may use at most 128 MiB of HBM per device.

v0:
```python
import functools

import jax
import jax.numpy as jnp
from jax import lax
from jax.sharding import Mesh
from jax.sharding import PartitionSpec as P

EXPERTS = 128
TOP_K = 8
CAP = 9
EXPERT = ("expert_0", "expert_1")
GROUPS_EXPERT = ("groups", "expert_0", "expert_1")


def in_blocks(shard, dim, peers):
    lengths = shard.shape
    pieces = shard.reshape(*lengths[:dim], peers, lengths[dim] // peers, *lengths[dim + 1 :])
    return jnp.moveaxis(pieces, dim, 0)


def cut_rows(length, count):
    unit = 8 if length >= 8 * count else 1
    return [length // unit * k // count * unit for k in range(1, count)]


def in_order(pieces, dim):
    pieces = jnp.moveaxis(pieces, 0, dim)
    lengths = pieces.shape
    return pieces.reshape(*lengths[:dim], lengths[dim] * lengths[dim + 1], *lengths[dim + 2 :])


def exchange_in_pieces(shard, axis, pieces, split_dim, concat_dim):
    blocks = in_blocks(shard, split_dim, lax.axis_size(axis))
    split_at = max(range(1, max(2, blocks.ndim - 1)), key=lambda d: blocks.shape[d])
    outs = []
    for section in jnp.split(blocks, cut_rows(blocks.shape[split_at], pieces), axis=split_at):
        if section.size:
            outs.append(lax.all_to_all(section, axis, split_axis=0, concat_axis=0, tiled=True))
    return in_order(jnp.concatenate(outs, axis=split_at), concat_dim)


def one_axis_at_a_time(shard, axes):
    return functools.reduce(lax.psum, axes, shard)


def on_device(tokens, router_weight, expert_ids):
    local_rows = tokens.shape[0]
    row_width = tokens.shape[1]
    logits = jnp.dot(tokens, router_weight, preferred_element_type=jnp.float32)
    probability = jax.nn.softmax(logits, axis=-1)
    gates = jax.nn.softmax(jnp.take_along_axis(logits, expert_ids, axis=1), axis=1)
    onehot = jnp.sum(
        (expert_ids[:, :, None] == jnp.arange(EXPERTS, dtype=jnp.int32)[None, None, :]).astype(
            jnp.int32
        ),
        axis=1,
    )
    before = jnp.cumsum(onehot, axis=0) - onehot
    slot_rank = jnp.take_along_axis(before, expert_ids, axis=1)
    slot_index = (expert_ids * CAP + slot_rank).reshape(-1)
    token_index = jnp.repeat(jnp.arange(local_rows, dtype=jnp.int32), TOP_K)
    slot_token = jnp.zeros((EXPERTS * CAP,), jnp.int32).at[slot_index].set(token_index)
    slot_gate = jnp.zeros((EXPERTS * CAP,), jnp.float32).at[slot_index].set(gates.reshape(-1))
    picked = tokens[slot_token]
    outgoing = (slot_gate[:, None] * picked.astype(jnp.float32)).astype(jnp.bfloat16)
    outgoing = outgoing.reshape(EXPERTS, CAP, row_width)
    expert_rows = exchange_in_pieces(outgoing, EXPERT, 2, 0, 1)
    expert_load = jnp.sum(onehot, axis=0).astype(jnp.float32)
    expert_mass = jnp.sum(probability, axis=0)
    token_total = jnp.float32(local_rows * lax.axis_size(EXPERT))
    load_all, mass_all = (
        one_axis_at_a_time(expert_load, EXPERT),
        one_axis_at_a_time(expert_mass, EXPERT),
    )
    summed = jnp.sum(load_all * mass_all)
    balance_loss = EXPERTS * summed / (token_total * token_total * TOP_K)
    return (expert_rows, balance_loss.reshape(1))


def solution(mesh):
    finer = Mesh(
        mesh.devices.reshape(mesh.shape["groups"], 32, 2), ("groups", "expert_0", "expert_1")
    )
    in_specs = (P(GROUPS_EXPERT, None), P(), P(GROUPS_EXPERT, None))
    out_specs = (P(EXPERT, "groups", None), P("groups"))
    return jax.shard_map(
        on_device, mesh=finer, in_specs=in_specs, out_specs=out_specs, check_vma=False
    )
```

profile of v0, /device:TPU:37, one launch (start us, length us, event | category | flops | bytes accessed | tf_op | source)
XLA Modules:
  0.0 1056.4 jit_solution(5879255299308648395)
XLA Ops:
  0.6 0.8 bitcast_or_fusion
  1.4 0.8 copy.39
  2.2 0.1 copy.40
  2.4 0.2 convert_reduce_fusion
  2.7 0.2 reduce_window_sum.11
  2.9 6.8 gather_fusion.1
  9.8 0.1 reshape.118
  9.9 0.6 fusion.8
  10.5 7.0 gather_fusion.2
  17.8 0.1 copy.44
  17.9 0.1 reshape.110
  18.0 0.1 copy.42
  18.1 0.1 reshape.81
  18.2 4.3 scatter_custom_fusion.1
  22.5 4.3 scatter_custom_fusion
  26.9 0.2 mul.22
  27.1 7.9 gather_fusion
  35.0 17.5 %reshape.85 = f32[64,2,9,4096]{3,2,1,0:T(8,128)} reshape(bf16[1152,4096]{1,0:T(8,128)(2,1)} %gather_fusion) | data formatting | bytes 28311552 | tf_op jit(solution)/shard_map/convert_element_type | solution.py:66
  52.5 18.0 %multiply_convert_fusion = bf16[64,2,9,4096]{3,2,1,0:T(8,128)(2,1)} fusion(f32[64,2,9,4096]{3,2,1,0:T(8,128)} %reshape.85, f32[64,2,9]{2,1,0:T(2,128)S(1)} %mul.22), kind=kLoop, calls=%fused_computation.5 | loop fusion | flops 9437184 | bytes 28316160 | tf_op jit(solution)/shard_map/convert_element_type | solution.py:66
  70.4 7.7 split.8
  78.1 34.4 %all-to-all-start = ((bf16[64,2,4,4096]{3,2,1,0:T(4,128)(2,1)}), bf16[64,2,4,4096]{3,2,1,0:T(4,128)(2,1)}, u32[]{:S(2)}, u32[]{:S(2)}) async-start(bf16[64,2,4,4096]{3,2,1,0:T(4,128)(2,1)} %split.8), calls=%async_computation | async-start | bytes 8388608 | tf_op jit(solution)/shard_map/all_to_all | solution.py:39
  112.5 7.3 split.9
  119.8 12.7 %copy.45 = bf16[64,2,5,4096]{3,1,2,0:T(2,128)(2,1)} copy(bf16[64,2,5,4096]{3,2,1,0:T(8,128)(2,1)S(1)} %split.9) | data formatting | bytes 10485760 | tf_op jit(solution)/shard_map/split | solution.py:37
  132.5 349.0 %all-to-all-done = bf16[64,2,4,4096]{3,2,1,0:T(4,128)(2,1)} async-done(((bf16[64,2,4,4096]{3,2,1,0:T(4,128)(2,1)}), bf16[64,2,4,4096]{3,2,1,0:T(4,128)(2,1)}, u32[]{:S(2)}, u32[]{:S(2)}) %all-to-all-start) | async-done | bytes 4194336 | tf_op jit(solution)/shard_map/all_to_all | solution.py:39
  481.5 17.1 %all-to-all-start.1 = ((bf16[64,2,5,4096]{3,1,2,0:T(2,128)(2,1)}), bf16[64,2,5,4096]{3,1,2,0:T(2,128)(2,1)}, u32[]{:S(2)}, u32[]{:S(2)}) async-start(bf16[64,2,5,4096]{3,1,2,0:T(2,128)(2,1)} %copy.45), calls=%async_computation.1 | async-start | bytes 10485760 | tf_op jit(solution)/shard_map/all_to_all | solution.py:39
  498.6 0.1 divide_reduce_fusion
  498.7 488.8 %all-reduce = (f32[128]{0:T(128)S(1)}, f32[128]{0:T(128)S(1)}) all-reduce(f32[128]{0:T(128)S(1)} %convert_element_type.21, f32[128]{0:T(128)S(1)} %divide_reduce_fusion), channel_id=1, replica_groups=mesh['groups'=4,'expert_0'=32,'expert_1'=2] {'expert_0'}, use_global_device_ids=true, to_apply=%region_7.8 | all-reduce | flops 256 | bytes 2048 | tf_op jit(solution)/shard_map/psum | solution.py:44
  987.5 17.8 %all-reduce.1 = (f32[128]{0:T(128)S(1)}, f32[128]{0:T(128)S(1)}) all-reduce(f32[128]{0:T(128)S(1)} %get-tuple-element.12, f32[128]{0:T(128)S(1)} %get-tuple-element.13), channel_id=1, replica_groups=mesh['groups'=4,'expert_0'=32,'expert_1'=2] {'expert_1'}, use_global_device_ids=true, to_apply=%region_8.9 | all-reduce | flops 256 | bytes 2048 | tf_op jit(solution)/shard_map/psum | solution.py:44
  1005.3 0.6 multiply_reduce_fusion
  1006.5 8.5 copy.46
  1015.1 25.9 %pad_maximum_fusion = bf16[64,2,9,4096]{3,1,2,0:T(2,128)(2,1)} fusion(bf16[64,2,5,4096]{3,1,2,0:T(2,128)(2,1)} %all-to-all-done.1, bf16[64,2,4,4096]{3,1,2,0:T(2,128)(2,1)} %copy.46), kind=kLoop, calls=%fused_computation.6 | loop fusion | flops 4718592 | bytes 18874368 | tf_op jit(solution)/shard_map/concatenate | solution.py:40
  1040.9 14.3 %copy.47 = bf16[2,576,4096]{2,1,0:T(8,128)(2,1)} copy(bf16[2,576,4096]{2,0,1:T(2,128)(2,1)} %bitcast.13) | data formatting | bytes 18874368
  (25 shorter events, 0.5 us)
Async XLA Ops:
  0.6 9.3 copy-start
  2.8 7.1 copy-start.2
  10.5 7.2 copy-start.3
  78.1 403.4 %all-to-all-start = ((bf16[64,2,4,4096]{3,2,1,0:T(4,128)(2,1)}), bf16[64,2,4,4096]{3,2,1,0:T(4,128)(2,1)}, u32[]{:S(2)}, u32[]{:S(2)}) async-start(bf16[64,2,4,4096]{3,2,1,0:T(4,128)(2,1)} %split.8), calls=%async_computation | async-start | bytes 8388608 | tf_op jit(solution)/shard_map/all_to_all | solution.py:39
  481.5 533.6 %all-to-all-start.1 = ((bf16[64,2,5,4096]{3,1,2,0:T(2,128)(2,1)}), bf16[64,2,5,4096]{3,1,2,0:T(2,128)(2,1)}, u32[]{:S(2)}, u32[]{:S(2)}) async-start(bf16[64,2,5,4096]{3,1,2,0:T(2,128)(2,1)} %copy.45), calls=%async_computation.1 | async-start | bytes 10485760 | tf_op jit(solution)/shard_map/all_to_all | solution.py:39
  1040.9 14.3 %copy-start.1 = (bf16[128,4096]{1,0:T(8,128)(2,1)S(1)}, bf16[128,4096]{1,0:T(8,128)(2,1)}, u32[]{:S(2)}) copy-start(bf16[128,4096]{1,0:T(8,128)(2,1)} %param.3) | copy-start | bytes 3145732
where the time goes:
time: 1060 us
  blocking collectives  507 us (48%)
  waiting for transfers between devices  349 us (33%)
  local copies, waits for them, and re-layouts  100 us (9%)
  starting transfers between devices  51.4 us (5%)
  other arithmetic  45.9 us (4%)
    psum x2, blocking collectives, one_axis_at_a_time(): return functools.reduce(lax.psum, axes, shard)  507 us
    all_to_all x2, waiting for transfers between devices, exchange_in_pieces(): lax.all_to_all(section, axis, split_axis=0, concat_axis=0, tiled=True)  349 us
    all_to_all x2, starting transfers between devices, exchange_in_pieces(): lax.all_to_all(section, axis, split_axis=0, concat_axis=0, tiled=True)  51.4 us
    split x3, local copies, waits for them, and re-layouts, exchange_in_pieces(): jnp.split(blocks, cut_rows(blocks.shape[split_at], pieces), axis=split_at)  27.7 us
    concatenate x1, other arithmetic, exchange_in_pieces(): return in_order(jnp.concatenate(outs, axis=split_at), concat_dim)  25.9 us
  transfers between devices with their start and end apart: 2, of which 1 were waited for; matrix products, arithmetic and copies ran while one was open for 3% of the time, Pallas kernels for 0%

commit v1 on v0

v1 whole, which is shorter than its diff:
```python
import functools

import jax
import jax.numpy as jnp
from jax import lax
from jax.experimental import pallas as pl
from jax.experimental.pallas import tpu as pltpu
from jax.sharding import Mesh
from jax.sharding import PartitionSpec as P

EXPERTS = 128
TOP_K = 8
CAP = 9
WIN = 24
EXPERT = ("chip", "core")
ALL = ("groups", "chip", "core")


def far_keys(away, reach, back):
    return [
        jnp.where((d >= 1) & (d <= r), d, 0).astype(jnp.float32)
        for d, r in ((away, reach), (away, reach - 1), (back, reach - 1), (back, reach))
    ]


def keys_of(ids, z, chips, per_chip, axis):
    away = lax.rem(ids // per_chip - z + chips, chips)
    back = lax.rem(chips - away, chips)
    return [
        jnp.max(k, axis=axis, keepdims=True) for k in far_keys(away, chips // 2, back)
    ]


def order_body(chips, per_chip, z_ref, ids_ref, idst_ref, tok_ref, *outs):
    rows, width = tok_ref.shape
    half = width // 2
    z = z_ref[0]
    cols = keys_of(ids_ref[...], z, chips, per_chip, 1)
    lanes = keys_of(idst_ref[...], z, chips, per_chip, 0)
    u = lax.broadcasted_iota(jnp.int32, (rows, rows), 0)
    t = lax.broadcasted_iota(jnp.int32, (rows, rows), 1)
    for which, (kc, kr) in enumerate(zip(cols, lanes)):
        ahead = (kc > kr) | ((kc == kr) & (u < t))
        place = jnp.sum(ahead.astype(jnp.float32), axis=0, keepdims=True)
        pick = (u.astype(jnp.float32) == place).astype(jnp.bfloat16)
        at = (which % 2) * half
        outs[which][...] = jnp.dot(
            pick, tok_ref[:, at : at + half], preferred_element_type=jnp.float32
        ).astype(jnp.bfloat16)


def route_body(chips, per_chip, z_ref, ids_ref, idst_ref, tok_ref, w_ref, tab_ref):
    rows = tok_ref.shape[0]
    reach = chips // 2
    z = z_ref[0]
    ids = ids_ref[...]
    logits = jnp.dot(tok_ref[...], w_ref[...], preferred_element_type=jnp.float32)
    e = lax.broadcasted_iota(jnp.int32, (rows, EXPERTS), 1)
    named = ids[:, 0:1] == e
    for k in range(1, TOP_K):
        named = named | (ids[:, k : k + 1] == e)
    top = jnp.max(logits, axis=1, keepdims=True)
    ex = jnp.exp(logits - top)
    probability = ex / jnp.sum(ex, axis=1, keepdims=True)
    best = jnp.max(jnp.where(named, logits, -jnp.inf), axis=1, keepdims=True)
    ge = jnp.exp(jnp.where(named, logits - best, -jnp.inf))
    gates = ge / jnp.sum(ge, axis=1, keepdims=True)
    count = named.astype(jnp.float32)
    u = lax.broadcasted_iota(jnp.int32, (rows, rows), 0)
    t = lax.broadcasted_iota(jnp.int32, (rows, rows), 1)
    lower = (t < u).astype(jnp.bfloat16)
    before = jnp.dot(lower, count.astype(jnp.bfloat16), preferred_element_type=jnp.float32)
    cols = keys_of(ids, z, chips, per_chip, 1)
    lanes = keys_of(idst_ref[...], z, chips, per_chip, 0)
    places = []
    for kc, kr in zip(cols, lanes):
        ahead = (kr > kc) | ((kr == kc) & (t < u))
        places.append(jnp.sum(ahead.astype(jnp.float32), axis=1, keepdims=True))
    away = lax.rem(e // per_chip - z + chips, chips)
    lo = jnp.where(away <= reach, places[0], places[2]) + 1.0
    hi = jnp.where(away < reach, places[1], places[3]) + 1.0
    for r in range(CAP):
        here = named & (before == r)
        for at, value, shift in ((0, lo, 1.0), (1, hi, 1.0), (2, gates, 0.0)):
            row = jnp.sum(jnp.where(here, value, 0.0), axis=0, keepdims=True) - shift
            tab_ref[at * CAP + r : at * CAP + r + 1, :] = row
    tab_ref[3 * CAP : 3 * CAP + 1, :] = jnp.sum(count, axis=0, keepdims=True)
    tab_ref[3 * CAP + 1 : 3 * CAP + 2, :] = jnp.sum(probability, axis=0, keepdims=True)
    tab_ref[3 * CAP + 2 :, :] = jnp.zeros((tab_ref.shape[0] - 3 * CAP - 2, EXPERTS), jnp.float32)


def place_body(plan, per_dev, sc_ref, *refs):
    n_src = len(plan)
    tabs = refs[:n_src]
    n_arr = 1 + max(i for src in plan for piece in src for i in piece)
    arrs = refs[n_src : n_src + n_arr]
    out_ref = refs[n_src + n_arr + 1]
    buf, sem = refs[n_src + n_arr + 2 :]
    core = sc_ref[n_src]
    wide = out_ref.shape[2]
    half = wide // 2
    step = 512

    def window(s, e):
        first = pl.multiple_of(((CAP * sc_ref[s]) // 4) * 8, 8)
        return out_ref.at[e, pl.ds(first, WIN), :]

    for s in range(n_src):
        for e in range(per_dev):
            k = s * per_dev + e
            pltpu.make_async_copy(window(s, e), buf.at[k], sem.at[k]).start()
    for s in range(n_src):
        for e in range(per_dev):
            k = s * per_dev + e
            pltpu.make_async_copy(window(s, e), buf.at[k], sem.at[k]).wait()
    for s in range(n_src):
        shift = lax.rem(2 * CAP * sc_ref[s], 8)
        w = lax.broadcasted_iota(jnp.int32, (WIN, step), 0) - shift
        mine = (w >= 0) & (w < 2 * CAP)
        for piece in range(2):
            own, peer = plan[s][piece]
            own_ref, peer_ref = arrs[own], arrs[peer]
            n = own_ref.shape[0]
            spot = tabs[s][0, :, piece : piece + 1]
            gate = tabs[s][0, :, 2:3]
            row = lax.broadcasted_iota(jnp.int32, (per_dev * WIN, n), 1).astype(jnp.float32)
            mine_f = (core * 128).astype(jnp.float32)
            peer_f = ((1 - core) * 128).astype(jnp.float32)
            s_own = (row == spot - mine_f).astype(jnp.bfloat16)
            s_peer = (row == spot - peer_f).astype(jnp.bfloat16)

            def column(i, carry, s=s, piece=piece, own_ref=own_ref, peer_ref=peer_ref,
                       s_own=s_own, s_peer=s_peer, gate=gate, mine=mine):
                c = pl.multiple_of(i * step, step)
                acc = jnp.dot(s_own, own_ref[:, pl.ds(c, step)], preferred_element_type=jnp.float32)
                acc = acc + jnp.dot(s_peer, peer_ref[:, pl.ds(c, step)], preferred_element_type=jnp.float32)
                acc = acc * gate
                at = pl.multiple_of(piece * half + i * step, step)
                for e in range(per_dev):
                    k = s * per_dev + e
                    old = buf[k, :, pl.ds(at, step)].astype(jnp.float32)
                    new = jnp.where(mine, acc[e * WIN : (e + 1) * WIN, :], old)
                    buf[k, :, pl.ds(at, step)] = new.astype(jnp.bfloat16)
                return carry

            lax.fori_loop(0, half // step, column, 0)
    for s in range(n_src):
        for e in range(per_dev):
            k = s * per_dev + e
            pltpu.make_async_copy(buf.at[k], window(s, e), sem.at[k]).start()
    for s in range(n_src):
        for e in range(per_dev):
            k = s * per_dev + e
            pltpu.make_async_copy(buf.at[k], window(s, e), sem.at[k]).wait()


def place(out, table, sources, core, plan, arrays):
    per_dev = out.shape[0]
    n_src = len(plan)
    scalars = jnp.stack([*sources, core]).astype(jnp.int32)

    def tab_spec(s):
        return pl.BlockSpec((1, *table.shape[1:]), lambda i, sc: (sc[s], 0, 0))

    whole = [pl.BlockSpec(a.shape, lambda i, sc: (0, 0)) for a in arrays]
    return pl.pallas_call(
        functools.partial(place_body, plan, per_dev),
        grid_spec=pltpu.PrefetchScalarGridSpec(
            num_scalar_prefetch=1,
            grid=(1,),
            in_specs=[*(tab_spec(s) for s in range(n_src)), *whole, pl.BlockSpec(memory_space=pl.ANY)],
            out_specs=pl.BlockSpec(memory_space=pl.ANY),
            scratch_shapes=[
                pltpu.VMEM((n_src * per_dev, WIN, out.shape[2]), out.dtype),
                pltpu.SemaphoreType.DMA((n_src * per_dev,)),
            ],
        ),
        out_shape=jax.ShapeDtypeStruct(out.shape, out.dtype),
        input_output_aliases={1 + n_src + len(arrays): 0},
        name="place",
    )(scalars, *([table] * n_src), *arrays, out)


def whole_call(body, scalar, arrays, shapes):
    spec = lambda a: pl.BlockSpec(a.shape, lambda: (0,) * len(a.shape))
    return pl.pallas_call(
        body,
        in_specs=[pl.BlockSpec(memory_space=pltpu.SMEM), *(spec(a) for a in arrays)],
        out_specs=[spec(s) for s in shapes],
        out_shape=shapes,
    )(scalar, *arrays)


def trade(message, totals, chips):
    core = lax.axis_index("core")
    z = lax.axis_index("chip")
    lanes = message.shape[-1]
    bits = chips.bit_length() - 1
    steps = [("core", 0, core)] + [("chip", k, z) for k in range(bits)]
    data = message.reshape(2 * chips, 1, lanes)
    blocks = 2 * chips
    seen = 1
    for axis, bit, index in steps:
        mine = (index >> bit) & 1
        data = data.reshape(blocks // 2, 2, seen, lanes)
        keep = lax.dynamic_index_in_dim(data, mine, 1, keepdims=False)
        give = lax.dynamic_index_in_dim(data, 1 - mine, 1, keepdims=False)
        rows = (blocks // 2) * seen
        packed = jnp.concatenate([give.reshape(rows, lanes), totals], axis=0)
        size = lax.axis_size(axis)
        got = lax.ppermute(packed, axis, [(i, i ^ (1 << bit)) for i in range(size)])
        totals = totals + got[rows:]
        came = got[:rows].reshape(blocks // 2, seen, lanes)
        low = jnp.where(mine == 0, keep, came)
        high = jnp.where(mine == 0, came, keep)
        data = jnp.stack([low, high], axis=1).reshape(blocks // 2, 2 * seen, lanes)
        blocks //= 2
        seen *= 2
    return data.reshape(seen, lanes), totals


def layer(tokens, router_weight, expert_ids):
    chips = lax.axis_size("chip")
    reach = chips // 2
    local_rows, width = tokens.shape
    half = width // 2
    per_dev = EXPERTS // (2 * chips)
    per_chip = 2 * per_dev
    slots_chip = per_chip * CAP
    z = lax.axis_index("chip")
    core = lax.axis_index("core")
    onward = [(i, (i + 1) % chips) for i in range(chips)]
    backward = [(i, (i - 1) % chips) for i in range(chips)]

    def send(x, to):
        return lax.ppermute(x, "chip", to)

    def swap(x):
        return lax.ppermute(x, "core", [(0, 1), (1, 0)])

    def need(h, far):
        rows = slots_chip * (far - h + 1)
        return min(local_rows, (rows + 7) // 8 * 8)

    ids_t = expert_ids.T
    zs = z.astype(jnp.int32).reshape(1)
    sds = jax.ShapeDtypeStruct
    flows = whole_call(
        functools.partial(order_body, chips, per_chip), zs,
        (expert_ids, ids_t, tokens), [sds((local_rows, half), tokens.dtype)] * 4,
    )
    (table,) = whole_call(
        functools.partial(route_body, chips, per_chip), zs,
        (expert_ids, ids_t, tokens, router_weight), [sds((32, EXPERTS), jnp.float32)],
    )
    rows = 3 * CAP
    message = table[:rows].reshape(rows, 2 * chips, per_dev).transpose(1, 2, 0)
    message = message.reshape(2 * chips, per_dev * rows)
    message = jnp.pad(message, ((0, 0), (0, 128 - per_dev * rows)))
    got, totals = trade(message, table[rows : rows + 2], chips)
    token_total = jnp.float32(local_rows * 2 * chips)
    loss = EXPERTS * jnp.sum(totals[0] * totals[1]) / (token_total * token_total * TOP_K)

    got = got[:, : per_dev * rows].reshape(chips, 2, per_dev, 3, CAP)
    bump = jnp.arange(2, dtype=jnp.float32)[None, :, None, None, None] * local_rows
    is_spot = (jnp.arange(3) < 2)[None, None, None, :, None]
    got = jnp.where(is_spot & (got >= 0), got + bump, got)
    got = got.transpose(0, 2, 1, 4, 3).reshape(chips // 4, 4, per_dev, 2 * CAP, 3)
    blank = jnp.array([-1.0, -1.0, 0.0], jnp.float32)
    moved = []
    for q in range(4):
        lead = (2 * CAP * q) % 8
        shape = lambda n: (chips // 4, per_dev, n, 3)
        moved.append(
            jnp.concatenate(
                [
                    jnp.broadcast_to(blank, shape(lead)),
                    got[:, q],
                    jnp.broadcast_to(blank, shape(WIN - lead - 2 * CAP)),
                ],
                axis=2,
            )
        )
    windows = jnp.stack(moved, axis=1).reshape(chips, per_dev * WIN, 3)
    windows = jnp.pad(windows, ((0, 0), (0, 0), (0, 5)))

    out = jnp.zeros((per_dev, 2 * chips * CAP, width), tokens.dtype)
    own = (flows[0], swap(flows[0]), flows[1], swap(flows[1]))
    out = place(out, windows, [z], core, (((0, 1), (2, 3)),), own)
    fars = (reach, reach - 1, reach - 1, reach)
    ways = (onward, onward, backward, backward)
    for h in range(1, reach + 1):
        up, down = (z - h) % chips, (z + h) % chips
        sent = []
        for x, far, way in zip(flows, fars, ways):
            if h <= far:
                x = send(x[: need(h, far)], way)
                sent.append(x)
            else:
                sent.append(None)
        flows = sent
        live = [x for x in flows if x is not None]
        arrays = tuple(y for x in live for y in (x, swap(x)))
        if h < reach:
            plan = (((0, 1), (2, 3)), ((4, 5), (6, 7)))
            out = place(out, windows, [up, down], core, plan, arrays)
        else:
            out = place(out, windows, [up], core, (((0, 1), (2, 3)),), arrays)
    return out, loss.reshape(1)


def solution(mesh):
    finer = Mesh(mesh.devices.reshape(mesh.shape["groups"], -1, 2), ALL)
    in_specs = (P(ALL, None), P(), P(ALL, None))
    out_specs = (P(EXPERT, "groups", None), P("groups"))
    return jax.shard_map(layer, mesh=finer, in_specs=in_specs, out_specs=out_specs, check_vma=False)
```

time: 1060 us -> 614 us (0.58)
  blocking collectives: 507 us -> 0 us
  starting transfers between devices: 51.4 us -> 188 us
  Pallas kernels: 0 us -> 136 us
  waiting for transfers between devices: 349 us -> 237 us
  local copies, waits for them, and re-layouts: 100 us -> 23.1 us
  other arithmetic: 45.9 us -> 14.8 us
    psum x2 -> x0, blocking collectives: 507 us -> none  [one_axis_at_a_time(): return functools.reduce(lax.psum, axes, shard)]
    all_to_all x2 -> x0, waiting for transfers between devices: 349 us -> none  [exchange_in_pieces(): lax.all_to_all(section, axis, split_axis=0, concat_axis=0, tiled=True)]
    ppermute x0 -> x132, waiting for transfers between devices: none -> 237 us  [the longest x62 201 us: send(): return lax.ppermute(x, 'chip', to)]
    ppermute x0 -> x132, starting transfers between devices: none -> 188 us  [the longest x64 79.6 us: swap(): return lax.ppermute(x, 'core', [(0, 1), (1, 0)])]
    pallas_call x0 -> x19, Pallas kernels: none -> 136 us  [the longest x17 130 us: place(): pl.pallas_call(functools.partial(place_body, plan, per_dev), grid_spec=pl...]
    all_to_all x2 -> x0, starting transfers between devices: 51.4 us -> none  [exchange_in_pieces(): lax.all_to_all(section, axis, split_axis=0, concat_axis=0, tiled=True)]
    split x3 -> x0, local copies, waits for them, and re-layouts: 27.7 us -> none  [exchange_in_pieces(): jnp.split(blocks, cut_rows(blocks.shape[split_at], pieces), axis=split_at)]
    concatenate x1 -> x6, other arithmetic: 25.9 us -> 0.04 us  [trade(): packed = jnp.concatenate([give.reshape(rows, lanes), totals], axis=0)]
  transfers between devices with their start and end apart: 2 -> 132, of which waited for: 1 -> 35; matrix products, arithmetic and copies ran while one was open for 3% -> 5% of each run, Pallas kernels for 0% -> 21%
where the time goes in v1:
time: 614 us; the launch traced here: 604 us
  waiting for transfers between devices  237 us (39%)
  starting transfers between devices  188 us (31%)
  Pallas kernels  136 us (22%)
  local copies, waits for them, and re-layouts  23.1 us (4%)
  other arithmetic  14.8 us (2%)
    ppermute x62, waiting for transfers between devices, send(): return lax.ppermute(x, 'chip', to)  201 us
    pallas_call x17, Pallas kernels, place(): pl.pallas_call(functools.partial(place_body, plan, per_dev), grid_spec=pl...  130 us
    ppermute x64, starting transfers between devices, swap(): return lax.ppermute(x, 'core', [(0, 1), (1, 0)])  79.6 us
    ppermute x62, starting transfers between devices, send(): return lax.ppermute(x, 'chip', to)  75.7 us
    ppermute x6, waiting for transfers between devices, trade(): got = lax.ppermute(packed, axis, [(i, i ^ 1 << bit) for i in range(size)])  35.8 us
    ppermute x6, starting transfers between devices, trade(): got = lax.ppermute(packed, axis, [(i, i ^ 1 << bit) for i in range(size)])  32.9 us
  transfers between devices with their start and end apart: 132, of which 35 were waited for; matrix products, arithmetic and copies ran while one was open for 5% of the time, Pallas kernels for 21%

profile of v1, /device:TPU:37, one launch (start us, length us, event | category | flops | bytes accessed | tf_op | source)
XLA Modules:
  0.0 604.0 jit_solution(4461537489441048734)
XLA Ops:
  6.7 20.5 %collective-permute-start = (f32[34,128]{1,0:T(8,128)S(1)}, f32[34,128]{1,0:T(8,128)S(1)}, u32[]{:S(2)}, u32[]{:S(2)}) collective-permute-start(f32[34,128]{1,0:T(8,128)S(1)} %pad_maximum_fusion.6), channel_id=1, source_target_pairs={{0,1},{1,0},{2,3},{3,2},{4,5},{5,4},{6,7},{7,6},{8,9},{9,8},{10,11... | collective-permute-start | bytes 52232 | tf_op jit(solution)/shard_map/ppermute | solution.py:211
  57.9 11.9 %collective-permute-start.5 = (f32[34,128]{1,0:T(8,128)S(1)}, f32[34,128]{1,0:T(8,128)}, u32[]{:S(2)}, u32[]{:S(2)}) collective-permute-start(f32[34,128]{1,0:T(8,128)S(1)} %pad_maximum_fusion.11), channel_id=1, source_target_pairs={{0,32},{2,34},{4,36},{6,38},{8,40},{10,42},{12,44},{14,46},{16,48}... | collective-permute-start | bytes 52232 | tf_op jit(solution)/shard_map/ppermute | solution.py:211
  69.7 22.2 %collective-permute-done.5 = f32[34,128]{1,0:T(8,128)} collective-permute-done((f32[34,128]{1,0:T(8,128)S(1)}, f32[34,128]{1,0:T(8,128)}, u32[]{:S(2)}, u32[]{:S(2)}) %collective-permute-start.5) | collective-permute-done | bytes 17440 | tf_op jit(solution)/shard_map/ppermute | solution.py:211
  95.8 10.8 %collective-permute-done.23.refs_8_ = bf16[128,2048]{1,0:T(8,128)(2,1)S(1)} collective-permute-done((bf16[128,2048]{1,0:T(8,128)(2,1)}, bf16[128,2048]{1,0:T(8,128)(2,1)S(1)}, u32[]{:S(2)}, u32[]{:S(2)}) %collective-permute-start.23) | collective-permute-done | bytes 524320 | tf_op jit(solution)/shard_map/ppermute | solution.py:236
  111.3 9.1 %collective-permute-done.42.refs_4_ = bf16[128,2048]{1,0:T(8,128)(2,1)S(1)} collective-permute-done((bf16[128,2048]{1,0:T(8,128)(2,1)S(1)}, bf16[128,2048]{1,0:T(8,128)(2,1)S(1)}, u32[]{:S(2)}, u32[]{:S(2)}) %collective-permute-start.42) | collective-permute-done | bytes 524320 | tf_op jit(solution)/shard_map/ppermute | solution.py:236
  139.8 10.2 %collective-permute-done.43.refs_4_ = bf16[128,2048]{1,0:T(8,128)(2,1)S(1)} collective-permute-done((bf16[128,2048]{1,0:T(8,128)(2,1)S(1)}, bf16[128,2048]{1,0:T(8,128)(2,1)S(1)}, u32[]{:S(2)}, u32[]{:S(2)}) %collective-permute-start.43) | collective-permute-done | bytes 524320 | tf_op jit(solution)/shard_map/ppermute | solution.py:236
  167.2 9.2 %collective-permute-done.44.refs_4_ = bf16[128,2048]{1,0:T(8,128)(2,1)S(1)} collective-permute-done((bf16[128,2048]{1,0:T(8,128)(2,1)S(1)}, bf16[128,2048]{1,0:T(8,128)(2,1)S(1)}, u32[]{:S(2)}, u32[]{:S(2)}) %collective-permute-start.44) | collective-permute-done | bytes 524320 | tf_op jit(solution)/shard_map/ppermute | solution.py:236
  194.2 9.2 %collective-permute-done.45.refs_4_ = bf16[128,2048]{1,0:T(8,128)(2,1)S(1)} collective-permute-done((bf16[128,2048]{1,0:T(8,128)(2,1)S(1)}, bf16[128,2048]{1,0:T(8,128)(2,1)S(1)}, u32[]{:S(2)}, u32[]{:S(2)}) %collective-permute-start.45) | collective-permute-done | bytes 524320 | tf_op jit(solution)/shard_map/ppermute | solution.py:236
  210.6 8.5 %collective-permute-done.11.refs_2_ = bf16[128,2048]{1,0:T(8,128)(2,1)} collective-permute-done((bf16[128,2048]{1,0:T(8,128)(2,1)S(1)}, bf16[128,2048]{1,0:T(8,128)(2,1)}, u32[]{:S(2)}, u32[]{:S(2)}) %collective-permute-start.11) | collective-permute-done | bytes 524320 | tf_op jit(solution)/shard_map/ppermute | solution.py:236
  221.2 9.2 %collective-permute-done.46.refs_4_ = bf16[128,2048]{1,0:T(8,128)(2,1)} collective-permute-done((bf16[128,2048]{1,0:T(8,128)(2,1)S(1)}, bf16[128,2048]{1,0:T(8,128)(2,1)}, u32[]{:S(2)}, u32[]{:S(2)}) %collective-permute-start.46) | collective-permute-done | bytes 524320 | tf_op jit(solution)/shard_map/ppermute | solution.py:236
  237.1 9.2 %collective-permute-done.12.refs_2_ = bf16[128,2048]{1,0:T(8,128)(2,1)} collective-permute-done((bf16[128,2048]{1,0:T(8,128)(2,1)}, bf16[128,2048]{1,0:T(8,128)(2,1)}, u32[]{:S(2)}, u32[]{:S(2)}) %collective-permute-start.12) | collective-permute-done | bytes 524320 | tf_op jit(solution)/shard_map/ppermute | solution.py:236
  248.4 9.1 %collective-permute-done.47.refs_4_ = bf16[128,2048]{1,0:T(8,128)(2,1)} collective-permute-done((bf16[128,2048]{1,0:T(8,128)(2,1)}, bf16[128,2048]{1,0:T(8,128)(2,1)}, u32[]{:S(2)}, u32[]{:S(2)}) %collective-permute-start.47) | collective-permute-done | bytes 524320 | tf_op jit(solution)/shard_map/ppermute | solution.py:236
  264.3 9.2 %collective-permute-done.13.refs_2_ = bf16[128,2048]{1,0:T(8,128)(2,1)} collective-permute-done((bf16[128,2048]{1,0:T(8,128)(2,1)}, bf16[128,2048]{1,0:T(8,128)(2,1)}, u32[]{:S(2)}, u32[]{:S(2)}) %collective-permute-start.13) | collective-permute-done | bytes 524320 | tf_op jit(solution)/shard_map/ppermute | solution.py:236
  275.8 9.0 %collective-permute-done.48.refs_4_ = bf16[128,2048]{1,0:T(8,128)(2,1)} collective-permute-done((bf16[128,2048]{1,0:T(8,128)(2,1)}, bf16[128,2048]{1,0:T(8,128)(2,1)}, u32[]{:S(2)}, u32[]{:S(2)}) %collective-permute-start.48) | collective-permute-done | bytes 524320 | tf_op jit(solution)/shard_map/ppermute | solution.py:236
  291.6 9.2 %collective-permute-done.14.refs_2_ = bf16[128,2048]{1,0:T(8,128)(2,1)} collective-permute-done((bf16[128,2048]{1,0:T(8,128)(2,1)}, bf16[128,2048]{1,0:T(8,128)(2,1)}, u32[]{:S(2)}, u32[]{:S(2)}) %collective-permute-start.14) | collective-permute-done | bytes 524320 | tf_op jit(solution)/shard_map/ppermute | solution.py:236
  302.9 9.1 %collective-permute-done.49.refs_4_ = bf16[128,2048]{1,0:T(8,128)(2,1)} collective-permute-done((bf16[128,2048]{1,0:T(8,128)(2,1)}, bf16[128,2048]{1,0:T(8,128)(2,1)}, u32[]{:S(2)}, u32[]{:S(2)}) %collective-permute-start.49) | collective-permute-done | bytes 524320 | tf_op jit(solution)/shard_map/ppermute | solution.py:236
  318.8 9.2 %collective-permute-done.15.refs_2_ = bf16[128,2048]{1,0:T(8,128)(2,1)} collective-permute-done((bf16[128,2048]{1,0:T(8,128)(2,1)}, bf16[128,2048]{1,0:T(8,128)(2,1)}, u32[]{:S(2)}, u32[]{:S(2)}) %collective-permute-start.15) | collective-permute-done | bytes 524320 | tf_op jit(solution)/shard_map/ppermute | solution.py:236
  330.1 9.1 %collective-permute-done.50.refs_4_ = bf16[128,2048]{1,0:T(8,128)(2,1)} collective-permute-done((bf16[128,2048]{1,0:T(8,128)(2,1)}, bf16[128,2048]{1,0:T(8,128)(2,1)}, u32[]{:S(2)}, u32[]{:S(2)}) %collective-permute-start.50) | collective-permute-done | bytes 524320 | tf_op jit(solution)/shard_map/ppermute | solution.py:236
  346.5 9.1 %collective-permute-done.16.refs_2_ = bf16[128,2048]{1,0:T(8,128)(2,1)} collective-permute-done((bf16[128,2048]{1,0:T(8,128)(2,1)}, bf16[128,2048]{1,0:T(8,128)(2,1)}, u32[]{:S(2)}, u32[]{:S(2)}) %collective-permute-start.16) | collective-permute-done | bytes 524320 | tf_op jit(solution)/shard_map/ppermute | solution.py:236
  357.8 9.0 %collective-permute-done.51.refs_4_ = bf16[128,2048]{1,0:T(8,128)(2,1)} collective-permute-done((bf16[128,2048]{1,0:T(8,128)(2,1)}, bf16[128,2048]{1,0:T(8,128)(2,1)}, u32[]{:S(2)}, u32[]{:S(2)}) %collective-permute-start.51) | collective-permute-done | bytes 524320 | tf_op jit(solution)/shard_map/ppermute | solution.py:236
  477.3 8.1 %place.18.refs_10_ = bf16[2,576,4096]{2,1,0:T(8,128)(2,1)} custom-call(s32[3]{0:T(128)} %add_add_fusion.14.sc_ref, f32[32,48,8]{2,1,0:T(8,128)} %pad.9.refs_0_.refs_1_, f32[32,48,8]{2,1,0:T(8,128)} %pad.9.refs_0_.refs_1_, bf16[128,2048]{1,0:T(8,128)(2,1)} %copy-done.7, bf16[128,2048]{1,0:T(8,128)(2,1)} %copy-done.13, ...), custom_call_target="tpu_custom_call", output_to_operand_aliasing={{}: (11, {})} | custom-call | tf_op jit(solution)/shard_map/place/pallas_call | solution.py:166
  485.4 8.1 %place.19.refs_10_ = bf16[2,576,4096]{2,1,0:T(8,128)(2,1)} custom-call(s32[3]{0:T(128)} %add_add_fusion.13.sc_ref, f32[32,48,8]{2,1,0:T(8,128)} %pad.9.refs_0_.refs_1_, f32[32,48,8]{2,1,0:T(8,128)} %pad.9.refs_0_.refs_1_, bf16[128,2048]{1,0:T(8,128)(2,1)} %copy-done.16, bf16[128,2048]{1,0:T(8,128)(2,1)} %copy-done.21, ...), custom_call_target="tpu_custom_call", output_to_operand_aliasing={{}: (11, {})} | custom-call | tf_op jit(solution)/shard_map/place/pallas_call | solution.py:166
  493.5 8.1 %place.20.refs_10_ = bf16[2,576,4096]{2,1,0:T(8,128)(2,1)} custom-call(s32[3]{0:T(128)} %add_add_fusion.12.sc_ref, f32[32,48,8]{2,1,0:T(8,128)} %pad.9.refs_0_.refs_1_, f32[32,48,8]{2,1,0:T(8,128)} %pad.9.refs_0_.refs_1_, bf16[128,2048]{1,0:T(8,128)(2,1)} %copy-done.24, bf16[128,2048]{1,0:T(8,128)(2,1)} %copy-done.29, ...), custom_call_target="tpu_custom_call", output_to_operand_aliasing={{}: (11, {})} | custom-call | tf_op jit(solution)/shard_map/place/pallas_call | solution.py:166
  501.6 8.1 %place.21.refs_10_ = bf16[2,576,4096]{2,1,0:T(8,128)(2,1)} custom-call(s32[3]{0:T(128)} %add_add_fusion.11.sc_ref, f32[32,48,8]{2,1,0:T(8,128)} %pad.9.refs_0_.refs_1_, f32[32,48,8]{2,1,0:T(8,128)} %pad.9.refs_0_.refs_1_, bf16[128,2048]{1,0:T(8,128)(2,1)} %copy-done.32, bf16[128,2048]{1,0:T(8,128)(2,1)} %copy-done.37, ...), custom_call_target="tpu_custom_call", output_to_operand_aliasing={{}: (11, {})} | custom-call | tf_op jit(solution)/shard_map/place/pallas_call | solution.py:166
  509.7 8.1 %place.22.refs_10_ = bf16[2,576,4096]{2,1,0:T(8,128)(2,1)} custom-call(s32[3]{0:T(128)} %add_add_fusion.10.sc_ref, f32[32,48,8]{2,1,0:T(8,128)} %pad.9.refs_0_.refs_1_, f32[32,48,8]{2,1,0:T(8,128)} %pad.9.refs_0_.refs_1_, bf16[128,2048]{1,0:T(8,128)(2,1)} %copy-done.40, bf16[128,2048]{1,0:T(8,128)(2,1)} %copy-done.45, ...), custom_call_target="tpu_custom_call", output_to_operand_aliasing={{}: (11, {})} | custom-call | tf_op jit(solution)/shard_map/place/pallas_call | solution.py:166
  517.8 8.1 %place.23.refs_10_ = bf16[2,576,4096]{2,1,0:T(8,128)(2,1)} custom-call(s32[3]{0:T(128)} %add_add_fusion.9.sc_ref, f32[32,48,8]{2,1,0:T(8,128)} %pad.9.refs_0_.refs_1_, f32[32,48,8]{2,1,0:T(8,128)} %pad.9.refs_0_.refs_1_, bf16[128,2048]{1,0:T(8,128)(2,1)} %collective-permute-done.11.refs_2_, ...), custom_call_target="tpu_custom_call", output_to_operand_aliasing={{}: (11, {})} | custom-call | tf_op jit(solution)/shard_map/place/pallas_call | solution.py:166
  525.9 8.1 %place.24.refs_10_ = bf16[2,576,4096]{2,1,0:T(8,128)(2,1)} custom-call(s32[3]{0:T(128)} %add_add_fusion.8.sc_ref, f32[32,48,8]{2,1,0:T(8,128)} %pad.9.refs_0_.refs_1_, f32[32,48,8]{2,1,0:T(8,128)} %pad.9.refs_0_.refs_1_, bf16[128,2048]{1,0:T(8,128)(2,1)} %collective-permute-done.12.refs_2_, ...), custom_call_target="tpu_custom_call", output_to_operand_aliasing={{}: (11, {})} | custom-call | tf_op jit(solution)/shard_map/place/pallas_call | solution.py:166
  534.0 8.1 %place.25.refs_10_ = bf16[2,576,4096]{2,1,0:T(8,128)(2,1)} custom-call(s32[3]{0:T(128)} %add_add_fusion.7.sc_ref, f32[32,48,8]{2,1,0:T(8,128)} %pad.9.refs_0_.refs_1_, f32[32,48,8]{2,1,0:T(8,128)} %pad.9.refs_0_.refs_1_, bf16[128,2048]{1,0:T(8,128)(2,1)} %collective-permute-done.13.refs_2_, ...), custom_call_target="tpu_custom_call", output_to_operand_aliasing={{}: (11, {})} | custom-call | tf_op jit(solution)/shard_map/place/pallas_call | solution.py:166
  542.1 8.1 %place.26.refs_10_ = bf16[2,576,4096]{2,1,0:T(8,128)(2,1)} custom-call(s32[3]{0:T(128)} %add_add_fusion.6.sc_ref, f32[32,48,8]{2,1,0:T(8,128)} %pad.9.refs_0_.refs_1_, f32[32,48,8]{2,1,0:T(8,128)} %pad.9.refs_0_.refs_1_, bf16[128,2048]{1,0:T(8,128)(2,1)} %collective-permute-done.14.refs_2_, ...), custom_call_target="tpu_custom_call", output_to_operand_aliasing={{}: (11, {})} | custom-call | tf_op jit(solution)/shard_map/place/pallas_call | solution.py:166
  550.2 8.1 %place.27.refs_10_ = bf16[2,576,4096]{2,1,0:T(8,128)(2,1)} custom-call(s32[3]{0:T(128)} %add_add_fusion.5.sc_ref, f32[32,48,8]{2,1,0:T(8,128)} %pad.9.refs_0_.refs_1_, f32[32,48,8]{2,1,0:T(8,128)} %pad.9.refs_0_.refs_1_, bf16[128,2048]{1,0:T(8,128)(2,1)} %collective-permute-done.15.refs_2_, ...), custom_call_target="tpu_custom_call", output_to_operand_aliasing={{}: (11, {})} | custom-call | tf_op jit(solution)/shard_map/place/pallas_call | solution.py:166
  558.3 8.1 %place.28.refs_10_ = bf16[2,576,4096]{2,1,0:T(8,128)(2,1)} custom-call(s32[3]{0:T(128)} %add_add_fusion.4.sc_ref, f32[32,48,8]{2,1,0:T(8,128)} %pad.9.refs_0_.refs_1_, f32[32,48,8]{2,1,0:T(8,128)} %pad.9.refs_0_.refs_1_, bf16[128,2048]{1,0:T(8,128)(2,1)} %collective-permute-done.16.refs_2_, ...), custom_call_target="tpu_custom_call", output_to_operand_aliasing={{}: (11, {})} | custom-call | tf_op jit(solution)/shard_map/place/pallas_call | solution.py:166
  566.4 8.1 %place.29.refs_10_ = bf16[2,576,4096]{2,1,0:T(8,128)(2,1)} custom-call(s32[3]{0:T(128)} %add_add_fusion.3.sc_ref, f32[32,48,8]{2,1,0:T(8,128)} %pad.9.refs_0_.refs_1_, f32[32,48,8]{2,1,0:T(8,128)} %pad.9.refs_0_.refs_1_, bf16[128,2048]{1,0:T(8,128)(2,1)} %collective-permute-done.17.refs_2_, ...), custom_call_target="tpu_custom_call", output_to_operand_aliasing={{}: (11, {})} | custom-call | tf_op jit(solution)/shard_map/place/pallas_call | solution.py:166
  (452 shorter events, 290.7 us)
Async XLA Ops:
  45.5 47.6 %collective-permute-start.130 = (bf16[128,2048]{1,0:T(8,128)(2,1)}, bf16[128,2048]{1,0:T(8,128)(2,1)S(1)}, u32[]{:S(2)}, u32[]{:S(2)}) collective-permute-start(bf16[128,2048]{1,0:T(8,128)(2,1)} %get-tuple-element.6.refs_1_), channel_id=1, source_target_pairs={{0,1},{1,0},{2,3},{3,2},{4,5},{5,4},{6,7},{7,6},{8,9},{9,8},{10,11... | collective-permute-start | bytes 1572872 | tf_op jit(solution)/shard_map/ppermute | solution.py:239
  49.1 44.0 %collective-permute-start.6 = (bf16[128,2048]{1,0:T(8,128)(2,1)}, bf16[128,2048]{1,0:T(8,128)(2,1)S(1)}, u32[]{:S(2)}, u32[]{:S(2)}) collective-permute-start(bf16[128,2048]{1,0:T(8,128)(2,1)} %get-tuple-element.6.refs_1_), channel_id=1, source_target_pairs={{0,2},{2,4},{4,6},{6,8},{8,10},{10,12},{12,14},{14,16},{16,18},{18... | collective-permute-start | bytes 1572872 | tf_op jit(solution)/shard_map/ppermute | solution.py:236
  50.2 43.1 %collective-permute-start.41 = (bf16[128,2048]{1,0:T(8,128)(2,1)}, bf16[128,2048]{1,0:T(8,128)(2,1)S(1)}, u32[]{:S(2)}, u32[]{:S(2)}) collective-permute-start(bf16[128,2048]{1,0:T(8,128)(2,1)} %get-tuple-element.8.refs_3_), channel_id=1, source_target_pairs={{0,2},{2,4},{4,6},{6,8},{8,10},{10,12},{12,14},{14,16},{16,18},{18... | collective-permute-start | bytes 1572872 | tf_op jit(solution)/shard_map/ppermute | solution.py:236
  51.4 42.3 %collective-permute-start.57 = (bf16[128,2048]{1,0:T(8,128)(2,1)}, bf16[128,2048]{1,0:T(8,128)(2,1)S(1)}, u32[]{:S(2)}, u32[]{:S(2)}) collective-permute-start(bf16[128,2048]{1,0:T(8,128)(2,1)} %get-tuple-element.9), channel_id=1, source_target_pairs={{0,62},{2,0},{4,2},{6,4},{8,6},{10,8},{12,10},{14,12},{16,14},{18,... | collective-permute-start | bytes 1572872 | tf_op jit(solution)/shard_map/ppermute | solution.py:236
  57.9 34.0 %collective-permute-start.5 = (f32[34,128]{1,0:T(8,128)S(1)}, f32[34,128]{1,0:T(8,128)}, u32[]{:S(2)}, u32[]{:S(2)}) collective-permute-start(f32[34,128]{1,0:T(8,128)S(1)} %pad_maximum_fusion.11), channel_id=1, source_target_pairs={{0,32},{2,34},{4,36},{6,38},{8,40},{10,42},{12,44},{14,46},{16,48}... | collective-permute-start | bytes 52232 | tf_op jit(solution)/shard_map/ppermute | solution.py:211
  177.8 25.5 %collective-permute-start.45 = (bf16[128,2048]{1,0:T(8,128)(2,1)S(1)}, bf16[128,2048]{1,0:T(8,128)(2,1)S(1)}, u32[]{:S(2)}, u32[]{:S(2)}) collective-permute-start(bf16[128,2048]{1,0:T(8,128)(2,1)S(1)} %collective-permute-done.44.refs_4_), channel_id=1, source_target_pairs={{0,2},{2,4},{4,6},{6,8},{8,10},{10,12},{12,14},{14,16},{16,18},{18... | collective-permute-start | bytes 1572872 | tf_op jit(solution)/shard_map/ppermute | solution.py:236
  178.6 25.9 %collective-permute-start.61 = (bf16[128,2048]{1,0:T(8,128)(2,1)S(1)}, bf16[128,2048]{1,0:T(8,128)(2,1)S(1)}, u32[]{:S(2)}, u32[]{:S(2)}) collective-permute-start(bf16[128,2048]{1,0:T(8,128)(2,1)S(1)} %collective-permute-done.60.refs_6_), channel_id=1, source_target_pairs={{0,62},{2,0},{4,2},{6,4},{8,6},{10,8},{12,10},{14,12},{16,14},{18,... | collective-permute-start | bytes 1572872 | tf_op jit(solution)/shard_map/ppermute | solution.py:236
  204.8 25.6 %collective-permute-start.46 = (bf16[128,2048]{1,0:T(8,128)(2,1)S(1)}, bf16[128,2048]{1,0:T(8,128)(2,1)}, u32[]{:S(2)}, u32[]{:S(2)}) collective-permute-start(bf16[128,2048]{1,0:T(8,128)(2,1)S(1)} %collective-permute-done.45.refs_4_), channel_id=1, source_target_pairs={{0,2},{2,4},{4,6},{6,8},{8,10},{10,12},{12,14},{14,16},{16,18},{18... | collective-permute-start | bytes 1572872 | tf_op jit(solution)/shard_map/ppermute | solution.py:236
  204.9 26.7 %collective-permute-start.62 = (bf16[128,2048]{1,0:T(8,128)(2,1)S(1)}, bf16[128,2048]{1,0:T(8,128)(2,1)}, u32[]{:S(2)}, u32[]{:S(2)}) collective-permute-start(bf16[128,2048]{1,0:T(8,128)(2,1)S(1)} %collective-permute-done.61.refs_6_), channel_id=1, source_target_pairs={{0,62},{2,0},{4,2},{6,4},{8,6},{10,8},{12,10},{14,12},{16,14},{18,... | collective-permute-start | bytes 1572872 | tf_op jit(solution)/shard_map/ppermute | solution.py:236
  207.6 24.1 %collective-permute-start.113 = (bf16[128,2048]{1,0:T(8,128)(2,1)S(1)}, bf16[128,2048]{1,0:T(8,128)(2,1)}, u32[]{:S(2)}, u32[]{:S(2)}) collective-permute-start(bf16[128,2048]{1,0:T(8,128)(2,1)S(1)} %collective-permute-done.27.refs_8_), channel_id=1, source_target_pairs={{0,1},{1,0},{2,3},{3,2},{4,5},{5,4},{6,7},{7,6},{8,9},{9,8},{10,11... | collective-permute-start | bytes 1572872 | tf_op jit(solution)/shard_map/ppermute | solution.py:239
  231.8 25.8 %collective-permute-start.47 = (bf16[128,2048]{1,0:T(8,128)(2,1)}, bf16[128,2048]{1,0:T(8,128)(2,1)}, u32[]{:S(2)}, u32[]{:S(2)}) collective-permute-start(bf16[128,2048]{1,0:T(8,128)(2,1)} %collective-permute-done.46.refs_4_), channel_id=1, source_target_pairs={{0,2},{2,4},{4,6},{6,8},{8,10},{10,12},{12,14},{14,16},{16,18},{18... | collective-permute-start | bytes 1572872 | tf_op jit(solution)/shard_map/ppermute | solution.py:236
  231.9 26.9 %collective-permute-start.63 = (bf16[128,2048]{1,0:T(8,128)(2,1)}, bf16[128,2048]{1,0:T(8,128)(2,1)}, u32[]{:S(2)}, u32[]{:S(2)}) collective-permute-start(bf16[128,2048]{1,0:T(8,128)(2,1)} %collective-permute-done.62.refs_6_), channel_id=1, source_target_pairs={{0,62},{2,0},{4,2},{6,4},{8,6},{10,8},{12,10},{14,12},{16,14},{18,... | collective-permute-start | bytes 1572872 | tf_op jit(solution)/shard_map/ppermute | solution.py:236
  234.6 24.3 %collective-permute-start.109 = (bf16[128,2048]{1,0:T(8,128)(2,1)}, bf16[128,2048]{1,0:T(8,128)(2,1)}, u32[]{:S(2)}, u32[]{:S(2)}) collective-permute-start(bf16[128,2048]{1,0:T(8,128)(2,1)} %collective-permute-done.28.refs_8_), channel_id=1, source_target_pairs={{0,1},{1,0},{2,3},{3,2},{4,5},{5,4},{6,7},{7,6},{8,9},{9,8},{10,11... | collective-permute-start | bytes 1572872 | tf_op jit(solution)/shard_map/ppermute | solution.py:239
  259.0 25.8 %collective-permute-start.48 = (bf16[128,2048]{1,0:T(8,128)(2,1)}, bf16[128,2048]{1,0:T(8,128)(2,1)}, u32[]{:S(2)}, u32[]{:S(2)}) collective-permute-start(bf16[128,2048]{1,0:T(8,128)(2,1)} %collective-permute-done.47.refs_4_), channel_id=1, source_target_pairs={{0,2},{2,4},{4,6},{6,8},{8,10},{10,12},{12,14},{14,16},{16,18},{18... | collective-permute-start | bytes 1572872 | tf_op jit(solution)/shard_map/ppermute | solution.py:236
  259.1 26.9 %collective-permute-start.64 = (bf16[128,2048]{1,0:T(8,128)(2,1)}, bf16[128,2048]{1,0:T(8,128)(2,1)}, u32[]{:S(2)}, u32[]{:S(2)}) collective-permute-start(bf16[128,2048]{1,0:T(8,128)(2,1)} %collective-permute-done.63.refs_6_), channel_id=1, source_target_pairs={{0,62},{2,0},{4,2},{6,4},{8,6},{10,8},{12,10},{14,12},{16,14},{18,... | collective-permute-start | bytes 1572872 | tf_op jit(solution)/shard_map/ppermute | solution.py:236
  261.8 24.3 %collective-permute-start.105 = (bf16[128,2048]{1,0:T(8,128)(2,1)}, bf16[128,2048]{1,0:T(8,128)(2,1)}, u32[]{:S(2)}, u32[]{:S(2)}) collective-permute-start(bf16[128,2048]{1,0:T(8,128)(2,1)} %collective-permute-done.29.refs_8_), channel_id=1, source_target_pairs={{0,1},{1,0},{2,3},{3,2},{4,5},{5,4},{6,7},{7,6},{8,9},{9,8},{10,11... | collective-permute-start | bytes 1572872 | tf_op jit(solution)/shard_map/ppermute | solution.py:239
  286.2 25.8 %collective-permute-start.49 = (bf16[128,2048]{1,0:T(8,128)(2,1)}, bf16[128,2048]{1,0:T(8,128)(2,1)}, u32[]{:S(2)}, u32[]{:S(2)}) collective-permute-start(bf16[128,2048]{1,0:T(8,128)(2,1)} %collective-permute-done.48.refs_4_), channel_id=1, source_target_pairs={{0,2},{2,4},{4,6},{6,8},{8,10},{10,12},{12,14},{14,16},{16,18},{18... | collective-permute-start | bytes 1572872 | tf_op jit(solution)/shard_map/ppermute | solution.py:236
  286.4 26.9 %collective-permute-start.65 = (bf16[128,2048]{1,0:T(8,128)(2,1)}, bf16[128,2048]{1,0:T(8,128)(2,1)}, u32[]{:S(2)}, u32[]{:S(2)}) collective-permute-start(bf16[128,2048]{1,0:T(8,128)(2,1)} %collective-permute-done.64.refs_6_), channel_id=1, source_target_pairs={{0,62},{2,0},{4,2},{6,4},{8,6},{10,8},{12,10},{14,12},{16,14},{18,... | collective-permute-start | bytes 1572872 | tf_op jit(solution)/shard_map/ppermute | solution.py:236
  289.0 24.3 %collective-permute-start.101 = (bf16[128,2048]{1,0:T(8,128)(2,1)}, bf16[128,2048]{1,0:T(8,128)(2,1)}, u32[]{:S(2)}, u32[]{:S(2)}) collective-permute-start(bf16[128,2048]{1,0:T(8,128)(2,1)} %collective-permute-done.30.refs_8_), channel_id=1, source_target_pairs={{0,1},{1,0},{2,3},{3,2},{4,5},{5,4},{6,7},{7,6},{8,9},{9,8},{10,11... | collective-permute-start | bytes 1572872 | tf_op jit(solution)/shard_map/ppermute | solution.py:239
  313.4 25.8 %collective-permute-start.50 = (bf16[128,2048]{1,0:T(8,128)(2,1)}, bf16[128,2048]{1,0:T(8,128)(2,1)}, u32[]{:S(2)}, u32[]{:S(2)}) collective-permute-start(bf16[128,2048]{1,0:T(8,128)(2,1)} %collective-permute-done.49.refs_4_), channel_id=1, source_target_pairs={{0,2},{2,4},{4,6},{6,8},{8,10},{10,12},{12,14},{14,16},{16,18},{18... | collective-permute-start | bytes 1572872 | tf_op jit(solution)/shard_map/ppermute | solution.py:236
  313.6 26.9 %collective-permute-start.66 = (bf16[128,2048]{1,0:T(8,128)(2,1)}, bf16[128,2048]{1,0:T(8,128)(2,1)}, u32[]{:S(2)}, u32[]{:S(2)}) collective-permute-start(bf16[128,2048]{1,0:T(8,128)(2,1)} %collective-permute-done.65.refs_6_), channel_id=1, source_target_pairs={{0,62},{2,0},{4,2},{6,4},{8,6},{10,8},{12,10},{14,12},{16,14},{18,... | collective-permute-start | bytes 1572872 | tf_op jit(solution)/shard_map/ppermute | solution.py:236
  316.2 24.3 %collective-permute-start.97 = (bf16[128,2048]{1,0:T(8,128)(2,1)}, bf16[128,2048]{1,0:T(8,128)(2,1)}, u32[]{:S(2)}, u32[]{:S(2)}) collective-permute-start(bf16[128,2048]{1,0:T(8,128)(2,1)} %collective-permute-done.31.refs_8_), channel_id=1, source_target_pairs={{0,1},{1,0},{2,3},{3,2},{4,5},{5,4},{6,7},{7,6},{8,9},{9,8},{10,11... | collective-permute-start | bytes 1572872 | tf_op jit(solution)/shard_map/ppermute | solution.py:239
  317.2 23.9 %collective-permute-start.32 = (bf16[128,2048]{1,0:T(8,128)(2,1)}, bf16[128,2048]{1,0:T(8,128)(2,1)}, u32[]{:S(2)}, u32[]{:S(2)}) collective-permute-start(bf16[128,2048]{1,0:T(8,128)(2,1)} %collective-permute-done.31.refs_8_), channel_id=1, source_target_pairs={{0,62},{2,0},{4,2},{6,4},{8,6},{10,8},{12,10},{14,12},{16,14},{18,... | collective-permute-start | bytes 1572872 | tf_op jit(solution)/shard_map/ppermute | solution.py:236
  341.1 25.8 %collective-permute-start.51 = (bf16[128,2048]{1,0:T(8,128)(2,1)}, bf16[128,2048]{1,0:T(8,128)(2,1)}, u32[]{:S(2)}, u32[]{:S(2)}) collective-permute-start(bf16[128,2048]{1,0:T(8,128)(2,1)} %collective-permute-done.50.refs_4_), channel_id=1, source_target_pairs={{0,2},{2,4},{4,6},{6,8},{8,10},{10,12},{12,14},{14,16},{16,18},{18... | collective-permute-start | bytes 1572872 | tf_op jit(solution)/shard_map/ppermute | solution.py:236
  341.2 25.6 %collective-permute-start.67 = (bf16[128,2048]{1,0:T(8,128)(2,1)}, bf16[128,2048]{1,0:T(8,128)(2,1)S(1)}, u32[]{:S(2)}, u32[]{:S(2)}) collective-permute-start(bf16[128,2048]{1,0:T(8,128)(2,1)} %collective-permute-done.66.refs_6_), channel_id=1, source_target_pairs={{0,62},{2,0},{4,2},{6,4},{8,6},{10,8},{12,10},{14,12},{16,14},{18,... | collective-permute-start | bytes 1572872 | tf_op jit(solution)/shard_map/ppermute | solution.py:236
  343.9 26.1 %collective-permute-start.93 = (bf16[128,2048]{1,0:T(8,128)(2,1)}, bf16[128,2048]{1,0:T(8,128)(2,1)S(1)}, u32[]{:S(2)}, u32[]{:S(2)}) collective-permute-start(bf16[128,2048]{1,0:T(8,128)(2,1)} %collective-permute-done.32.refs_8_), channel_id=1, source_target_pairs={{0,1},{1,0},{2,3},{3,2},{4,5},{5,4},{6,7},{7,6},{8,9},{9,8},{10,11... | collective-permute-start | bytes 1572872 | tf_op jit(solution)/shard_map/ppermute | solution.py:239
  344.9 27.0 %collective-permute-start.33 = (bf16[128,2048]{1,0:T(8,128)(2,1)}, bf16[128,2048]{1,0:T(8,128)(2,1)}, u32[]{:S(2)}, u32[]{:S(2)}) collective-permute-start(bf16[128,2048]{1,0:T(8,128)(2,1)} %collective-permute-done.32.refs_8_), channel_id=1, source_target_pairs={{0,62},{2,0},{4,2},{6,4},{8,6},{10,8},{12,10},{14,12},{16,14},{18,... | collective-permute-start | bytes 1572872 | tf_op jit(solution)/shard_map/ppermute | solution.py:236
  457.8 132.3 %collective-permute-start.40 = (bf16[72,2048]{1,0:T(8,128)(2,1)}, bf16[72,2048]{1,0:T(8,128)(2,1)}, u32[]{:S(2)}, u32[]{:S(2)}) collective-permute-start(bf16[72,2048]{1,0:T(8,128)(2,1)} %collective-permute-done.20.refs_2_), channel_id=1, source_target_pairs={{0,1},{1,0},{2,3},{3,2},{4,5},{5,4},{6,7},{7,6},{8,9},{9,8},{10,11... | collective-permute-start | bytes 884744 | tf_op jit(solution)/shard_map/ppermute | solution.py:239
  461.3 128.8 %collective-permute-start.73 = (bf16[72,2048]{1,0:T(8,128)(2,1)}, bf16[72,2048]{1,0:T(8,128)(2,1)}, u32[]{:S(2)}, u32[]{:S(2)}) collective-permute-start(bf16[72,2048]{1,0:T(8,128)(2,1)} %collective-permute-done.37.refs_8_), channel_id=1, source_target_pairs={{0,1},{1,0},{2,3},{3,2},{4,5},{5,4},{6,7},{7,6},{8,9},{9,8},{10,11... | collective-permute-start | bytes 884744 | tf_op jit(solution)/shard_map/ppermute | solution.py:239
  462.7 127.3 %collective-permute-start.72 = (bf16[40,2048]{1,0:T(8,128)(2,1)}, bf16[40,2048]{1,0:T(8,128)(2,1)}, u32[]{:S(2)}, u32[]{:S(2)}) collective-permute-start(bf16[40,2048]{1,0:T(8,128)(2,1)} %collective-permute-done.71.refs_6_), channel_id=1, source_target_pairs={{0,1},{1,0},{2,3},{3,2},{4,5},{5,4},{6,7},{7,6},{8,9},{9,8},{10,11... | collective-permute-start | bytes 491528 | tf_op jit(solution)/shard_map/ppermute | solution.py:239
  462.9 134.4 %collective-permute-start.22 = (bf16[40,2048]{1,0:T(8,128)(2,1)}, bf16[40,2048]{1,0:T(8,128)(2,1)}, u32[]{:S(2)}, u32[]{:S(2)}) collective-permute-start(bf16[40,2048]{1,0:T(8,128)(2,1)} %collective-permute-done.21.refs_1_), channel_id=1, source_target_pairs={{0,1},{1,0},{2,3},{3,2},{4,5},{5,4},{6,7},{7,6},{8,9},{9,8},{10,11... | collective-permute-start | bytes 491528 | tf_op jit(solution)/shard_map/ppermute | solution.py:239
  463.4 133.9 %collective-permute-start.39 = (bf16[40,2048]{1,0:T(8,128)(2,1)}, bf16[40,2048]{1,0:T(8,128)(2,1)}, u32[]{:S(2)}, u32[]{:S(2)}) collective-permute-start(bf16[40,2048]{1,0:T(8,128)(2,1)} %collective-permute-done.38.refs_3_), channel_id=1, source_target_pairs={{0,1},{1,0},{2,3},{3,2},{4,5},{5,4},{6,7},{7,6},{8,9},{9,8},{10,11... | collective-permute-start | bytes 491528 | tf_op jit(solution)/shard_map/ppermute | solution.py:239
  (157 other events, 10846.3 us)

commit v2 on v1

v2 whole, which is shorter than its diff:
```python
import functools

import jax
import jax.numpy as jnp
from jax import lax
from jax.experimental import pallas as pl
from jax.experimental.pallas import tpu as pltpu
from jax.sharding import Mesh
from jax.sharding import PartitionSpec as P

EXPERTS = 128
TOP_K = 8
CAP = 9
WIN = 24
EXPERT = ("chip", "core")
ALL = ("groups", "chip", "core")


def far_keys(away, reach, back):
    return [
        jnp.where((d >= 1) & (d <= r), d, 0).astype(jnp.float32)
        for d, r in ((away, reach), (away, reach - 1), (back, reach - 1), (back, reach))
    ]


def keys_of(ids, z, chips, per_chip, axis):
    away = lax.rem(ids // per_chip - z + chips, chips)
    back = lax.rem(chips - away, chips)
    return [
        jnp.max(k, axis=axis, keepdims=True) for k in far_keys(away, chips // 2, back)
    ]


def order_body(chips, per_chip, z_ref, ids_ref, idst_ref, tok_ref, *outs):
    rows, width = tok_ref.shape
    half = width // 2
    z = z_ref[0]
    cols = keys_of(ids_ref[...], z, chips, per_chip, 1)
    lanes = keys_of(idst_ref[...], z, chips, per_chip, 0)
    u = lax.broadcasted_iota(jnp.int32, (rows, rows), 0)
    t = lax.broadcasted_iota(jnp.int32, (rows, rows), 1)
    for which, (kc, kr) in enumerate(zip(cols, lanes)):
        ahead = (kc > kr) | ((kc == kr) & (u < t))
        place = jnp.sum(ahead.astype(jnp.float32), axis=0, keepdims=True)
        pick = (u.astype(jnp.float32) == place).astype(jnp.bfloat16)
        at = (which % 2) * half
        outs[which][...] = jnp.dot(
            pick, tok_ref[:, at : at + half], preferred_element_type=jnp.float32
        ).astype(jnp.bfloat16)


def route_body(chips, per_chip, z_ref, ids_ref, idst_ref, tok_ref, w_ref, tab_ref):
    rows = tok_ref.shape[0]
    reach = chips // 2
    z = z_ref[0]
    ids = ids_ref[...]
    logits = jnp.dot(tok_ref[...], w_ref[...], preferred_element_type=jnp.float32)
    e = lax.broadcasted_iota(jnp.int32, (rows, EXPERTS), 1)
    named = ids[:, 0:1] == e
    for k in range(1, TOP_K):
        named = named | (ids[:, k : k + 1] == e)
    top = jnp.max(logits, axis=1, keepdims=True)
    ex = jnp.exp(logits - top)
    probability = ex / jnp.sum(ex, axis=1, keepdims=True)
    best = jnp.max(jnp.where(named, logits, -jnp.inf), axis=1, keepdims=True)
    ge = jnp.exp(jnp.where(named, logits - best, -jnp.inf))
    gates = ge / jnp.sum(ge, axis=1, keepdims=True)
    count = named.astype(jnp.float32)
    u = lax.broadcasted_iota(jnp.int32, (rows, rows), 0)
    t = lax.broadcasted_iota(jnp.int32, (rows, rows), 1)
    lower = (t < u).astype(jnp.bfloat16)
    before = jnp.dot(lower, count.astype(jnp.bfloat16), preferred_element_type=jnp.float32)
    cols = keys_of(ids, z, chips, per_chip, 1)
    lanes = keys_of(idst_ref[...], z, chips, per_chip, 0)
    places = []
    for kc, kr in zip(cols, lanes):
        ahead = (kr > kc) | ((kr == kc) & (t < u))
        places.append(jnp.sum(ahead.astype(jnp.float32), axis=1, keepdims=True))
    away = lax.rem(e // per_chip - z + chips, chips)
    lo = jnp.where(away <= reach, places[0], places[2]) + 1.0
    hi = jnp.where(away < reach, places[1], places[3]) + 1.0
    for r in range(CAP):
        here = named & (before == r)
        for at, value, shift in ((0, lo, 1.0), (1, hi, 1.0), (2, gates, 0.0)):
            row = jnp.sum(jnp.where(here, value, 0.0), axis=0, keepdims=True) - shift
            tab_ref[at * CAP + r : at * CAP + r + 1, :] = row
    tab_ref[3 * CAP : 3 * CAP + 1, :] = jnp.sum(count, axis=0, keepdims=True)
    tab_ref[3 * CAP + 1 : 3 * CAP + 2, :] = jnp.sum(probability, axis=0, keepdims=True)
    tab_ref[3 * CAP + 2 :, :] = jnp.zeros((tab_ref.shape[0] - 3 * CAP - 2, EXPERTS), jnp.float32)


def place_body(n_src, n_old, fresh, per_dev, sc_ref, *refs):
    refs = list(refs)
    take = lambda n: [refs.pop(0) for _ in range(n)]
    tabs, flows = take(n_src), take(2 * n_src)
    keep_old, got_old = take(2) if n_old else (None, None)
    if n_old and not fresh:
        take(1)
    (out_ref,) = take(1) if n_old else (None,)
    keep_ref, give_ref = take(2) if n_src else (None, None)
    step = 512
    span = per_dev * WIN
    if n_old:
        buf, in_sem, out_sem = refs
        wide = out_ref.shape[2]
        spots = [(s, e) for s in range(n_old) for e in range(per_dev)]

        def window(s, e):
            first = pl.multiple_of(((CAP * sc_ref[n_src + s]) // 4) * 8, 8)
            return out_ref.at[e, pl.ds(first, WIN), :]

        def fetch(sources):
            for k, (s, e) in enumerate(spots):
                if s in sources:
                    pltpu.make_async_copy(window(s, e), buf.at[k], in_sem.at[k]).start()

        def settle(sources):
            for k, (s, e) in enumerate(spots):
                if s in sources:
                    pltpu.make_async_copy(buf.at[k], window(s, e), out_sem.at[k]).wait()

        fetch((0, 1))
        for k, (s, e) in enumerate(spots):
            if s == 2 and e == 0:
                settle((0, 1))
                fetch((2,))
            pltpu.make_async_copy(window(s, e), buf.at[k], in_sem.at[k]).wait()
            shift = lax.rem(2 * CAP * sc_ref[n_src + s], 8)
            w = lax.broadcasted_iota(jnp.int32, (WIN, step), 0) - shift
            mine = (w >= 0) & (w < 2 * CAP)

            def merge(i, carry, k=k, mine=mine):
                c = pl.multiple_of(i * step, step)
                here = (pl.ds(k * WIN, WIN), pl.ds(c, step))
                new = keep_old[here].astype(jnp.float32) + got_old[here].astype(jnp.float32)
                old = buf[k, :, pl.ds(c, step)].astype(jnp.float32)
                buf[k, :, pl.ds(c, step)] = jnp.where(mine, new, old).astype(buf.dtype)
                return carry

            lax.fori_loop(0, wide // step, merge, 0)
            pltpu.make_async_copy(buf.at[k], window(s, e), out_sem.at[k]).start()
    for s in range(n_src):
        for piece in range(2):
            flow = flows[2 * s + piece]
            n, half = flow.shape
            spot = tabs[s][0, :, piece : piece + 1]
            gate = tabs[s][0, :, 2:3]
            row = lax.broadcasted_iota(jnp.int32, (2 * span, n), 1).astype(jnp.float32)
            pick = (row == spot).astype(jnp.bfloat16)

            def column(i, carry, s=s, piece=piece, flow=flow, pick=pick, gate=gate, half=half):
                c = pl.multiple_of(i * step, step)
                acc = jnp.dot(pick, flow[:, pl.ds(c, step)], preferred_element_type=jnp.float32)
                acc = (acc * gate).astype(jnp.bfloat16)
                at = pl.multiple_of(piece * half + i * step, step)
                keep_ref[s * span : (s + 1) * span, pl.ds(at, step)] = acc[:span]
                give_ref[s * span : (s + 1) * span, pl.ds(at, step)] = acc[span:]
                return carry

            lax.fori_loop(0, half // step, column, 0)
    if n_old:
        settle((2,) if n_old > 2 else (0, 1))


def place(out, table, sources, flows, old, shape, per_dev):
    n_src = len(sources)
    n_old = len(old[0]) if old else 0
    fresh = out is None
    span = per_dev * WIN
    width = shape.shape[2]
    scalars = jnp.stack([*sources, *(old[0] if old else ())]).astype(jnp.int32)
    flat = lambda a: pl.BlockSpec(a.shape, lambda i, sc: (0, 0))
    anywhere = pl.BlockSpec(memory_space=pl.ANY)
    args, specs, outs, out_specs, scratch, alias = [], [], [], [], [], {}
    for s in range(n_src):
        args.append(table)
        specs.append(pl.BlockSpec((1, *table.shape[1:]), lambda i, sc, s=s: (sc[s], 0, 0)))
    for a in (*flows, *(old[1:] if old else ())):
        args.append(a)
        specs.append(flat(a))
    if n_old:
        if not fresh:
            alias = {1 + len(args): 0}
            args.append(out)
            specs.append(anywhere)
        outs.append(shape)
        out_specs.append(anywhere)
        count = n_old * per_dev
        scratch = [
            pltpu.VMEM((count, WIN, width), shape.dtype),
            pltpu.SemaphoreType.DMA((count,)),
            pltpu.SemaphoreType.DMA((count,)),
        ]
    if n_src:
        block = jax.ShapeDtypeStruct((n_src * span, width), shape.dtype)
        outs += [block, block]
        out_specs += [flat(block), flat(block)]
    result = pl.pallas_call(
        functools.partial(place_body, n_src, n_old, fresh, per_dev),
        grid_spec=pltpu.PrefetchScalarGridSpec(
            num_scalar_prefetch=1, grid=(1,), in_specs=specs, out_specs=out_specs,
            scratch_shapes=scratch,
        ),
        out_shape=outs,
        input_output_aliases=alias,
        name="place",
    )(scalars, *args)
    result = list(result)
    if n_old:
        out = result.pop(0)
    return out, result


def whole_call(body, scalar, arrays, shapes):
    spec = lambda a: pl.BlockSpec(a.shape, lambda: (0,) * len(a.shape))
    return pl.pallas_call(
        body,
        in_specs=[pl.BlockSpec(memory_space=pltpu.SMEM), *(spec(a) for a in arrays)],
        out_specs=[spec(s) for s in shapes],
        out_shape=shapes,
    )(scalar, *arrays)


def trade(message, totals, chips):
    z = lax.axis_index("chip")
    lanes = message.shape[-1]
    data = message
    blocks, seen = chips, 1
    for step in range(chips.bit_length() - 1):
        mine = (z >> step) & 1
        data = data.reshape(blocks // 2, 2, seen, lanes)
        keep = lax.dynamic_index_in_dim(data, mine, 1, keepdims=False)
        give = lax.dynamic_index_in_dim(data, 1 - mine, 1, keepdims=False)
        rows = chips // 2
        packed = jnp.concatenate([give.reshape(rows, lanes), totals], axis=0)
        got = lax.ppermute(packed, "chip", [(i, i ^ (1 << step)) for i in range(chips)])
        totals = totals + got[rows:]
        came = got[:rows].reshape(blocks // 2, seen, lanes)
        low = jnp.where(mine == 0, keep, came)
        high = jnp.where(mine == 0, came, keep)
        data = jnp.stack([low, high], axis=1)
        blocks //= 2
        seen *= 2
    totals = totals + lax.ppermute(totals, "core", [(0, 1), (1, 0)])
    return data.reshape(chips, lanes), totals


def layer(tokens, router_weight, expert_ids):
    chips = lax.axis_size("chip")
    reach = chips // 2
    local_rows, width = tokens.shape
    half = width // 2
    per_dev = EXPERTS // (2 * chips)
    per_chip = 2 * per_dev
    slots_chip = per_chip * CAP
    z = lax.axis_index("chip")
    core = lax.axis_index("core")
    onward = [(i, (i + 1) % chips) for i in range(chips)]
    backward = [(i, (i - 1) % chips) for i in range(chips)]

    def send(x, to):
        return lax.ppermute(x, "chip", to)

    def swap(x):
        return lax.ppermute(x, "core", [(0, 1), (1, 0)])

    def need(h, far):
        if h <= reach - 3:
            return local_rows
        rows = slots_chip * (far - h + 1)
        return min(local_rows, (rows + 7) // 8 * 8)

    ids_t = expert_ids.T
    zs = z.astype(jnp.int32).reshape(1)
    sds = jax.ShapeDtypeStruct
    flows = whole_call(
        functools.partial(order_body, chips, per_chip), zs,
        (expert_ids, ids_t, tokens), [sds((local_rows, half), tokens.dtype)] * 4,
    )
    (table,) = whole_call(
        functools.partial(route_body, chips, per_chip), zs,
        (expert_ids, ids_t, tokens, router_weight), [sds((32, EXPERTS), jnp.float32)],
    )
    rows = 3 * CAP
    message = table[:rows].reshape(rows, chips, per_chip).transpose(1, 2, 0)
    message = message.reshape(chips, per_chip * rows)
    message = jnp.pad(message, ((0, 0), (0, 128 - per_chip * rows)))
    got, totals = trade(message, table[rows : rows + 2], chips)
    token_total = jnp.float32(local_rows * 2 * chips)
    loss = EXPERTS * jnp.sum(totals[0] * totals[1]) / (token_total * token_total * TOP_K)

    blank = jnp.array([-1.0, -1.0, 0.0], jnp.float32)
    got = got[:, : per_chip * rows].reshape(chips, 2, per_dev, 3, CAP)
    got = jnp.where(core == 0, got, got[:, ::-1]).reshape(chips, per_chip, 3, CAP)
    got = got.transpose(0, 1, 3, 2)
    void = jnp.broadcast_to(blank, got.shape)
    got = jnp.concatenate(
        [jnp.where(core == 0, got, void), jnp.where(core == 0, void, got)], axis=2
    ).reshape(chips // 4, 4, per_chip, 2 * CAP, 3)
    moved = []
    for q in range(4):
        lead = (2 * CAP * q) % 8
        shape = lambda n: (chips // 4, per_chip, n, 3)
        moved.append(
            jnp.concatenate(
                [
                    jnp.broadcast_to(blank, shape(lead)),
                    got[:, q],
                    jnp.broadcast_to(blank, shape(WIN - lead - 2 * CAP)),
                ],
                axis=2,
            )
        )
    windows = jnp.stack(moved, axis=1).reshape(chips, per_chip * WIN, 3)
    windows = jnp.pad(windows, ((0, 0), (0, 0), (0, 5)))

    shape = sds((per_dev, 2 * chips * CAP, width), tokens.dtype)
    out, (keep, give) = place(None, windows, [z], flows[:2], None, shape, per_dev)
    old = ([z], keep, swap(give))
    fars = (reach, reach - 1, reach - 1, reach)
    ways = (onward, onward, backward, backward)
    live, sources = [], []
    for h in range(1, reach + 1):
        up, down = (z - h) % chips, (z + h) % chips
        sent = []
        for x, far, way in zip(flows, fars, ways):
            if h <= far:
                x = send(x[: need(h, far)], way)
                sent.append(x)
            else:
                sent.append(None)
        flows = sent
        live += [x for x in flows if x is not None]
        sources += [up, down] if h < reach else [up]
        if h == reach - 1:
            continue
        out, (keep, give) = place(out, windows, sources, live, old, shape, per_dev)
        old = (sources, keep, swap(give))
        live, sources = [], []
    out, _ = place(out, windows, [], [], old, shape, per_dev)
    return out, loss.reshape(1)


def solution(mesh):
    finer = Mesh(mesh.devices.reshape(mesh.shape["groups"], -1, 2), ALL)
    in_specs = (P(ALL, None), P(), P(ALL, None))
    out_specs = (P(EXPERT, "groups", None), P("groups"))
    return jax.shard_map(layer, mesh=finer, in_specs=in_specs, out_specs=out_specs, check_vma=False)
```

time: 614 us -> 640 us (1.042)
  waiting for transfers between devices: 237 us -> 280 us
  starting transfers between devices: 188 us -> 156 us
  local copies, waits for them, and re-layouts: 23.1 us -> 36.3 us
  Pallas kernels: 136 us -> 143 us
    ppermute x62, waiting for transfers between devices: 201 us -> 273 us  [send(): return lax.ppermute(x, 'chip', to)]
    ppermute x64 -> x16, starting transfers between devices: 79.6 us -> 31.5 us  [swap(): return lax.ppermute(x, 'core', [(0, 1), (1, 0)])]
    ppermute x6, waiting for transfers between devices: 35.8 us -> 6.3 us  [the longest x5 4.39 us: trade(): lax.ppermute(packed, 'chip', [(i, i ^ 1 << step) for i in range(chips)])]
    unnamed x116 -> x157, local copies, waits for them, and re-layouts: 2.76 us -> 20.8 us
    ppermute x6, starting transfers between devices: 32.9 us -> 50.8 us  [the longest x5 50.6 us: trade(): lax.ppermute(packed, 'chip', [(i, i ^ 1 << step) for i in range(chips)])]
  transfers between devices with their start and end apart: 132 -> 84, of which waited for: 35 -> 41; matrix products, arithmetic and copies ran while one was open for 5% -> 4% of each run, Pallas kernels for 21% -> 1%
where the time goes in v2:
time: 640 us; the launch traced here: 631 us
  waiting for transfers between devices  280 us (44%)
  starting transfers between devices  156 us (24%)
  Pallas kernels  143 us (22%)
  local copies, waits for them, and re-layouts  36.3 us (6%)
  other arithmetic  12 us (2%)
    ppermute x62, waiting for transfers between devices, send(): return lax.ppermute(x, 'chip', to)  273 us
    pallas_call x17, Pallas kernels, place(): pl.pallas_call(functools.partial(place_body, n_src, n_old, fresh, per_dev...  136 us
    ppermute x62, starting transfers between devices, send(): return lax.ppermute(x, 'chip', to)  73.9 us
    ppermute x5, starting transfers between devices, trade(): lax.ppermute(packed, 'chip', [(i, i ^ 1 << step) for i in range(chips)])  50.6 us
    ppermute x16, starting transfers between devices, swap(): return lax.ppermute(x, 'core', [(0, 1), (1, 0)])  31.5 us
    unnamed x157, local copies, waits for them, and re-layouts  20.8 us
  transfers between devices with their start and end apart: 84, of which 41 were waited for; matrix products, arithmetic and copies ran while one was open for 4% of the time, Pallas kernels for 1%

profile of v2, /device:TPU:37, one launch (start us, length us, event | category | flops | bytes accessed | tf_op | source)
XLA Modules:
  0.0 630.5 jit_solution(1102225182279382305)
XLA Ops:
  25.0 15.3 %collective-permute-start.3 = (f32[18,128]{1,0:T(8,128)S(1)}, f32[18,128]{1,0:T(8,128)S(1)}, u32[]{:S(2)}, u32[]{:S(2)}) collective-permute-start(f32[18,128]{1,0:T(8,128)S(1)} %pad_maximum_fusion.8), channel_id=1, source_target_pairs={{0,16},{2,18},{4,20},{6,22},{8,24},{10,26},{12,28},{14,30},{16,0},... | collective-permute-start | bytes 27656 | tf_op jit(solution)/shard_map/ppermute | solution.py:236
  41.4 21.4 %collective-permute-start.4 = (f32[18,128]{1,0:T(8,128)S(1)}, f32[18,128]{1,0:T(8,128)S(1)}, u32[]{:S(2)}, u32[]{:S(2)}) collective-permute-start(f32[18,128]{1,0:T(8,128)S(1)} %pad_maximum_fusion.9), channel_id=1, source_target_pairs={{0,32},{2,34},{4,36},{6,38},{8,40},{10,42},{12,44},{14,46},{16,48}... | collective-permute-start | bytes 27656 | tf_op jit(solution)/shard_map/ppermute | solution.py:236
  79.4 9.5 %collective-permute-start.67 = (bf16[48,4096]{1,0:T(8,128)(2,1)}, bf16[48,4096]{1,0:T(8,128)(2,1)S(1)}, u32[]{:S(2)}, u32[]{:S(2)}) collective-permute-start(bf16[48,4096]{1,0:T(8,128)(2,1)} %get-tuple-element.58), channel_id=1, source_target_pairs={{0,1},{1,0},{2,3},{3,2},{4,5},{5,4},{6,7},{7,6},{8,9},{9,8},{10,11... | collective-permute-start | bytes 1179656 | tf_op jit(solution)/shard_map/ppermute | solution.py:265
  108.3 9.7 %collective-permute-done.21.refs_3_ = bf16[128,2048]{1,0:T(8,128)(2,1)S(1)} collective-permute-done((bf16[128,2048]{1,0:T(8,128)(2,1)}, bf16[128,2048]{1,0:T(8,128)(2,1)S(1)}, u32[]{:S(2)}, u32[]{:S(2)}) %collective-permute-start.21) | collective-permute-done | bytes 524320 | tf_op jit(solution)/shard_map/ppermute | solution.py:262
  118.1 11.2 %collective-permute-done.6.refs_2_ = bf16[128,2048]{1,0:T(8,128)(2,1)S(1)} collective-permute-done((bf16[128,2048]{1,0:T(8,128)(2,1)}, bf16[128,2048]{1,0:T(8,128)(2,1)S(1)}, u32[]{:S(2)}, u32[]{:S(2)}) %collective-permute-start.6) | collective-permute-done | bytes 524320 | tf_op jit(solution)/shard_map/ppermute | solution.py:262
  130.9 8.4 %place.19 = (bf16[2,576,4096]{2,1,0:T(8,128)(2,1)}, bf16[96,4096]{1,0:T(8,128)(2,1)}, bf16[96,4096]{1,0:T(8,128)(2,1)}) custom-call(s32[4]{0:T(128)} %pad_add_fusion.13.sc_ref, f32[32,96,8]{2,1,0:T(8,128)} %pad.9.refs_0_.refs_1_.refs_2_, f32[32,96,8]{2,1,0:T(8,128)} %pad.9.refs_0_.refs_1_.refs_2_, ...), custom_call_target="tpu_custom_call", output_to_operand_aliasing={{0}: (9, {})} | custom-call | tf_op jit(solution)/shard_map/place/pallas_call | solution.py:198
  145.5 10.0 %collective-permute-done.22.refs_3_ = bf16[128,2048]{1,0:T(8,128)(2,1)S(1)} collective-permute-done((bf16[128,2048]{1,0:T(8,128)(2,1)}, bf16[128,2048]{1,0:T(8,128)(2,1)S(1)}, u32[]{:S(2)}, u32[]{:S(2)}) %collective-permute-start.22) | collective-permute-done | bytes 524320 | tf_op jit(solution)/shard_map/ppermute | solution.py:262
  155.5 11.2 %collective-permute-done.7.refs_2_ = bf16[128,2048]{1,0:T(8,128)(2,1)S(1)} collective-permute-done((bf16[128,2048]{1,0:T(8,128)(2,1)}, bf16[128,2048]{1,0:T(8,128)(2,1)S(1)}, u32[]{:S(2)}, u32[]{:S(2)}) %collective-permute-start.7) | collective-permute-done | bytes 524320 | tf_op jit(solution)/shard_map/ppermute | solution.py:262
  183.5 10.3 %collective-permute-done.23.refs_3_ = bf16[128,2048]{1,0:T(8,128)(2,1)S(1)} collective-permute-done((bf16[128,2048]{1,0:T(8,128)(2,1)}, bf16[128,2048]{1,0:T(8,128)(2,1)S(1)}, u32[]{:S(2)}, u32[]{:S(2)}) %collective-permute-start.23) | collective-permute-done | bytes 524320 | tf_op jit(solution)/shard_map/ppermute | solution.py:262
  193.8 11.2 %collective-permute-done.8.refs_2_ = bf16[128,2048]{1,0:T(8,128)(2,1)S(1)} collective-permute-done((bf16[128,2048]{1,0:T(8,128)(2,1)}, bf16[128,2048]{1,0:T(8,128)(2,1)S(1)}, u32[]{:S(2)}, u32[]{:S(2)}) %collective-permute-start.8) | collective-permute-done | bytes 524320 | tf_op jit(solution)/shard_map/ppermute | solution.py:262
  221.5 10.0 %collective-permute-done.24.refs_3_ = bf16[128,2048]{1,0:T(8,128)(2,1)S(1)} collective-permute-done((bf16[128,2048]{1,0:T(8,128)(2,1)}, bf16[128,2048]{1,0:T(8,128)(2,1)S(1)}, u32[]{:S(2)}, u32[]{:S(2)}) %collective-permute-start.24) | collective-permute-done | bytes 524320 | tf_op jit(solution)/shard_map/ppermute | solution.py:262
  231.5 11.2 %collective-permute-done.9.refs_2_ = bf16[128,2048]{1,0:T(8,128)(2,1)S(1)} collective-permute-done((bf16[128,2048]{1,0:T(8,128)(2,1)}, bf16[128,2048]{1,0:T(8,128)(2,1)S(1)}, u32[]{:S(2)}, u32[]{:S(2)}) %collective-permute-start.9) | collective-permute-done | bytes 524320 | tf_op jit(solution)/shard_map/ppermute | solution.py:262
  259.5 10.3 %collective-permute-done.10.refs_2_ = bf16[128,2048]{1,0:T(8,128)(2,1)S(1)} collective-permute-done((bf16[128,2048]{1,0:T(8,128)(2,1)}, bf16[128,2048]{1,0:T(8,128)(2,1)S(1)}, u32[]{:S(2)}, u32[]{:S(2)}) %collective-permute-start.10) | collective-permute-done | bytes 524320 | tf_op jit(solution)/shard_map/ppermute | solution.py:262
  269.8 11.2 %collective-permute-done.25.refs_3_ = bf16[128,2048]{1,0:T(8,128)(2,1)S(1)} collective-permute-done((bf16[128,2048]{1,0:T(8,128)(2,1)}, bf16[128,2048]{1,0:T(8,128)(2,1)S(1)}, u32[]{:S(2)}, u32[]{:S(2)}) %collective-permute-start.25) | collective-permute-done | bytes 524320 | tf_op jit(solution)/shard_map/ppermute | solution.py:262
  297.0 10.3 %collective-permute-done.11.refs_2_ = bf16[128,2048]{1,0:T(8,128)(2,1)S(1)} collective-permute-done((bf16[128,2048]{1,0:T(8,128)(2,1)}, bf16[128,2048]{1,0:T(8,128)(2,1)S(1)}, u32[]{:S(2)}, u32[]{:S(2)}) %collective-permute-start.11) | collective-permute-done | bytes 524320 | tf_op jit(solution)/shard_map/ppermute | solution.py:262
  307.2 11.2 %collective-permute-done.26.refs_3_ = bf16[128,2048]{1,0:T(8,128)(2,1)S(1)} collective-permute-done((bf16[128,2048]{1,0:T(8,128)(2,1)}, bf16[128,2048]{1,0:T(8,128)(2,1)S(1)}, u32[]{:S(2)}, u32[]{:S(2)}) %collective-permute-start.26) | collective-permute-done | bytes 524320 | tf_op jit(solution)/shard_map/ppermute | solution.py:262
  335.0 10.1 %collective-permute-done.12.refs_2_ = bf16[128,2048]{1,0:T(8,128)(2,1)S(1)} collective-permute-done((bf16[128,2048]{1,0:T(8,128)(2,1)}, bf16[128,2048]{1,0:T(8,128)(2,1)S(1)}, u32[]{:S(2)}, u32[]{:S(2)}) %collective-permute-start.12) | collective-permute-done | bytes 524320 | tf_op jit(solution)/shard_map/ppermute | solution.py:262
  345.0 11.2 %collective-permute-done.27.refs_3_ = bf16[128,2048]{1,0:T(8,128)(2,1)S(1)} collective-permute-done((bf16[128,2048]{1,0:T(8,128)(2,1)}, bf16[128,2048]{1,0:T(8,128)(2,1)S(1)}, u32[]{:S(2)}, u32[]{:S(2)}) %collective-permute-start.27) | collective-permute-done | bytes 524320 | tf_op jit(solution)/shard_map/ppermute | solution.py:262
  357.7 8.4 %place.25 = (bf16[2,576,4096]{2,1,0:T(8,128)(2,1)}, bf16[96,4096]{1,0:T(8,128)(2,1)}, bf16[96,4096]{1,0:T(8,128)(2,1)}) custom-call(s32[4]{0:T(128)} %pad_add_fusion.7.sc_ref, f32[32,96,8]{2,1,0:T(8,128)} %pad.9.refs_0_.refs_1_.refs_2_, f32[32,96,8]{2,1,0:T(8,128)} %pad.9.refs_0_.refs_1_.refs_2_, ...), custom_call_target="tpu_custom_call", output_to_operand_aliasing={{0}: (9, {})} | custom-call | tf_op jit(solution)/shard_map/place/pallas_call | solution.py:198
  372.8 10.2 %collective-permute-done.13.refs_2_ = bf16[128,2048]{1,0:T(8,128)(2,1)S(1)} collective-permute-done((bf16[128,2048]{1,0:T(8,128)(2,1)}, bf16[128,2048]{1,0:T(8,128)(2,1)S(1)}, u32[]{:S(2)}, u32[]{:S(2)}) %collective-permute-start.13) | collective-permute-done | bytes 524320 | tf_op jit(solution)/shard_map/ppermute | solution.py:262
  383.0 11.2 %collective-permute-done.28.refs_3_ = bf16[128,2048]{1,0:T(8,128)(2,1)S(1)} collective-permute-done((bf16[128,2048]{1,0:T(8,128)(2,1)}, bf16[128,2048]{1,0:T(8,128)(2,1)S(1)}, u32[]{:S(2)}, u32[]{:S(2)}) %collective-permute-start.28) | collective-permute-done | bytes 524320 | tf_op jit(solution)/shard_map/ppermute | solution.py:262
  409.7 9.9 %collective-permute-done.14.refs_2_ = bf16[128,2048]{1,0:T(8,128)(2,1)S(1)} collective-permute-done((bf16[128,2048]{1,0:T(8,128)(2,1)}, bf16[128,2048]{1,0:T(8,128)(2,1)S(1)}, u32[]{:S(2)}, u32[]{:S(2)}) %collective-permute-start.14) | collective-permute-done | bytes 524320 | tf_op jit(solution)/shard_map/ppermute | solution.py:262
  419.7 11.2 %collective-permute-done.29.refs_3_ = bf16[128,2048]{1,0:T(8,128)(2,1)S(1)} collective-permute-done((bf16[128,2048]{1,0:T(8,128)(2,1)}, bf16[128,2048]{1,0:T(8,128)(2,1)S(1)}, u32[]{:S(2)}, u32[]{:S(2)}) %collective-permute-start.29) | collective-permute-done | bytes 524320 | tf_op jit(solution)/shard_map/ppermute | solution.py:262
  432.4 8.4 %place.27 = (bf16[2,576,4096]{2,1,0:T(8,128)(2,1)}, bf16[96,4096]{1,0:T(8,128)(2,1)}, bf16[96,4096]{1,0:T(8,128)(2,1)}) custom-call(s32[4]{0:T(128)} %pad_add_fusion.5.sc_ref, f32[32,96,8]{2,1,0:T(8,128)} %pad.9.refs_0_.refs_1_.refs_2_, f32[32,96,8]{2,1,0:T(8,128)} %pad.9.refs_0_.refs_1_.refs_2_, ...), custom_call_target="tpu_custom_call", output_to_operand_aliasing={{0}: (9, {})} | custom-call | tf_op jit(solution)/shard_map/place/pallas_call | solution.py:198
  447.8 10.2 %collective-permute-done.15.refs_2_ = bf16[128,2048]{1,0:T(8,128)(2,1)S(1)} collective-permute-done((bf16[128,2048]{1,0:T(8,128)(2,1)}, bf16[128,2048]{1,0:T(8,128)(2,1)S(1)}, u32[]{:S(2)}, u32[]{:S(2)}) %collective-permute-start.15) | collective-permute-done | bytes 524320 | tf_op jit(solution)/shard_map/ppermute | solution.py:262
  458.0 11.2 %collective-permute-done.30.refs_3_ = bf16[128,2048]{1,0:T(8,128)(2,1)S(1)} collective-permute-done((bf16[128,2048]{1,0:T(8,128)(2,1)}, bf16[128,2048]{1,0:T(8,128)(2,1)S(1)}, u32[]{:S(2)}, u32[]{:S(2)}) %collective-permute-start.30) | collective-permute-done | bytes 524320 | tf_op jit(solution)/shard_map/ppermute | solution.py:262
  484.7 9.9 %collective-permute-done.16.refs_2_ = bf16[128,2048]{1,0:T(8,128)(2,1)S(1)} collective-permute-done((bf16[128,2048]{1,0:T(8,128)(2,1)}, bf16[128,2048]{1,0:T(8,128)(2,1)S(1)}, u32[]{:S(2)}, u32[]{:S(2)}) %collective-permute-start.16) | collective-permute-done | bytes 524320 | tf_op jit(solution)/shard_map/ppermute | solution.py:262
  494.7 11.2 %collective-permute-done.31.refs_3_ = bf16[128,2048]{1,0:T(8,128)(2,1)S(1)} collective-permute-done((bf16[128,2048]{1,0:T(8,128)(2,1)}, bf16[128,2048]{1,0:T(8,128)(2,1)S(1)}, u32[]{:S(2)}, u32[]{:S(2)}) %collective-permute-start.31) | collective-permute-done | bytes 524320 | tf_op jit(solution)/shard_map/ppermute | solution.py:262
  522.4 9.8 %collective-permute-done.17.refs_2_ = bf16[128,2048]{1,0:T(8,128)(2,1)S(1)} collective-permute-done((bf16[128,2048]{1,0:T(8,128)(2,1)}, bf16[128,2048]{1,0:T(8,128)(2,1)S(1)}, u32[]{:S(2)}, u32[]{:S(2)}) %collective-permute-start.17) | collective-permute-done | bytes 524320 | tf_op jit(solution)/shard_map/ppermute | solution.py:262
  532.1 11.2 %collective-permute-done.32.refs_3_ = bf16[128,2048]{1,0:T(8,128)(2,1)S(1)} collective-permute-done((bf16[128,2048]{1,0:T(8,128)(2,1)}, bf16[128,2048]{1,0:T(8,128)(2,1)S(1)}, u32[]{:S(2)}, u32[]{:S(2)}) %collective-permute-start.32) | collective-permute-done | bytes 524320 | tf_op jit(solution)/shard_map/ppermute | solution.py:262
  565.9 9.6 %collective-permute-done.33.refs_3_ = bf16[72,2048]{1,0:T(8,128)(2,1)S(1)} collective-permute-done((bf16[72,2048]{1,0:T(8,128)(2,1)S(1)}, bf16[72,2048]{1,0:T(8,128)(2,1)S(1)}, u32[]{:S(2)}, u32[]{:S(2)}) %collective-permute-start.33) | collective-permute-done | bytes 294944 | tf_op jit(solution)/shard_map/ppermute | solution.py:262
  605.9 9.8 %place.32 = (bf16[2,576,4096]{2,1,0:T(8,128)(2,1)}, bf16[144,4096]{1,0:T(8,128)(2,1)}, bf16[144,4096]{1,0:T(8,128)(2,1)}) custom-call(s32[5]{0:T(128)} %stack.228.sc_ref, f32[32,96,8]{2,1,0:T(8,128)} %pad.9.refs_0_.refs_1_.refs_2_, f32[32,96,8]{2,1,0:T(8,128)} %pad.9.refs_0_.refs_1_.refs_2_, ...), custom_call_target="tpu_custom_call", output_to_operand_aliasing={{0}: (12, {})} | custom-call | tf_op jit(solution)/shard_map/place/pallas_call | solution.py:198
  (387 shorter events, 280.9 us)
Async XLA Ops:
  41.4 28.5 %collective-permute-start.4 = (f32[18,128]{1,0:T(8,128)S(1)}, f32[18,128]{1,0:T(8,128)S(1)}, u32[]{:S(2)}, u32[]{:S(2)}) collective-permute-start(f32[18,128]{1,0:T(8,128)S(1)} %pad_maximum_fusion.9), channel_id=1, source_target_pairs={{0,32},{2,34},{4,36},{6,38},{8,40},{10,42},{12,44},{14,46},{16,48}... | collective-permute-start | bytes 27656 | tf_op jit(solution)/shard_map/ppermute | solution.py:236
  99.5 30.4 %collective-permute-start.68 = (bf16[96,4096]{1,0:T(8,128)(2,1)}, bf16[96,4096]{1,0:T(8,128)(2,1)S(1)}, u32[]{:S(2)}, u32[]{:S(2)}) collective-permute-start(bf16[96,4096]{1,0:T(8,128)(2,1)} %get-tuple-element.60), channel_id=1, source_target_pairs={{0,1},{1,0},{2,3},{3,2},{4,5},{5,4},{6,7},{7,6},{8,9},{9,8},{10,11... | collective-permute-start | bytes 2359304 | tf_op jit(solution)/shard_map/ppermute | solution.py:265
  103.9 25.4 %collective-permute-start.6 = (bf16[128,2048]{1,0:T(8,128)(2,1)}, bf16[128,2048]{1,0:T(8,128)(2,1)S(1)}, u32[]{:S(2)}, u32[]{:S(2)}) collective-permute-start(bf16[128,2048]{1,0:T(8,128)(2,1)} %copy-done.26), channel_id=1, source_target_pairs={{0,2},{2,4},{4,6},{6,8},{8,10},{10,12},{12,14},{14,16},{16,18},{18... | collective-permute-start | bytes 1572872 | tf_op jit(solution)/shard_map/ppermute | solution.py:262
  139.4 28.0 %collective-permute-start.69 = (bf16[96,4096]{1,0:T(8,128)(2,1)}, bf16[96,4096]{1,0:T(8,128)(2,1)S(1)}, u32[]{:S(2)}, u32[]{:S(2)}) collective-permute-start(bf16[96,4096]{1,0:T(8,128)(2,1)} %get-tuple-element.63), channel_id=1, source_target_pairs={{0,1},{1,0},{2,3},{3,2},{4,5},{5,4},{6,7},{7,6},{8,9},{9,8},{10,11... | collective-permute-start | bytes 2359304 | tf_op jit(solution)/shard_map/ppermute | solution.py:265
  176.8 28.7 %collective-permute-start.70 = (bf16[96,4096]{1,0:T(8,128)(2,1)}, bf16[96,4096]{1,0:T(8,128)(2,1)S(1)}, u32[]{:S(2)}, u32[]{:S(2)}) collective-permute-start(bf16[96,4096]{1,0:T(8,128)(2,1)} %get-tuple-element.66), channel_id=1, source_target_pairs={{0,1},{1,0},{2,3},{3,2},{4,5},{5,4},{6,7},{7,6},{8,9},{9,8},{10,11... | collective-permute-start | bytes 2359304 | tf_op jit(solution)/shard_map/ppermute | solution.py:265
  179.6 25.4 %collective-permute-start.8 = (bf16[128,2048]{1,0:T(8,128)(2,1)}, bf16[128,2048]{1,0:T(8,128)(2,1)S(1)}, u32[]{:S(2)}, u32[]{:S(2)}) collective-permute-start(bf16[128,2048]{1,0:T(8,128)(2,1)} %copy-done.34), channel_id=1, source_target_pairs={{0,2},{2,4},{4,6},{6,8},{8,10},{10,12},{12,14},{14,16},{16,18},{18... | collective-permute-start | bytes 1572872 | tf_op jit(solution)/shard_map/ppermute | solution.py:262
  179.7 25.3 %collective-permute-start.38 = (bf16[128,2048]{1,0:T(8,128)(2,1)}, bf16[128,2048]{1,0:T(8,128)(2,1)S(1)}, u32[]{:S(2)}, u32[]{:S(2)}) collective-permute-start(bf16[128,2048]{1,0:T(8,128)(2,1)} %copy-done.35), channel_id=1, source_target_pairs={{0,62},{2,0},{4,2},{6,4},{8,6},{10,8},{12,10},{14,12},{16,14},{18,... | collective-permute-start | bytes 1572872 | tf_op jit(solution)/shard_map/ppermute | solution.py:262
  215.0 28.3 %collective-permute-start.71 = (bf16[96,4096]{1,0:T(8,128)(2,1)}, bf16[96,4096]{1,0:T(8,128)(2,1)S(1)}, u32[]{:S(2)}, u32[]{:S(2)}) collective-permute-start(bf16[96,4096]{1,0:T(8,128)(2,1)} %get-tuple-element.69), channel_id=1, source_target_pairs={{0,1},{1,0},{2,3},{3,2},{4,5},{5,4},{6,7},{7,6},{8,9},{9,8},{10,11... | collective-permute-start | bytes 2359304 | tf_op jit(solution)/shard_map/ppermute | solution.py:265
  252.7 28.4 %collective-permute-start.72 = (bf16[96,4096]{1,0:T(8,128)(2,1)}, bf16[96,4096]{1,0:T(8,128)(2,1)S(1)}, u32[]{:S(2)}, u32[]{:S(2)}) collective-permute-start(bf16[96,4096]{1,0:T(8,128)(2,1)} %get-tuple-element.72), channel_id=1, source_target_pairs={{0,1},{1,0},{2,3},{3,2},{4,5},{5,4},{6,7},{7,6},{8,9},{9,8},{10,11... | collective-permute-start | bytes 2359304 | tf_op jit(solution)/shard_map/ppermute | solution.py:265
  255.6 25.5 %collective-permute-start.25 = (bf16[128,2048]{1,0:T(8,128)(2,1)}, bf16[128,2048]{1,0:T(8,128)(2,1)S(1)}, u32[]{:S(2)}, u32[]{:S(2)}) collective-permute-start(bf16[128,2048]{1,0:T(8,128)(2,1)} %copy-done.28), channel_id=1, source_target_pairs={{0,2},{2,4},{4,6},{6,8},{8,10},{10,12},{12,14},{14,16},{16,18},{18... | collective-permute-start | bytes 1572872 | tf_op jit(solution)/shard_map/ppermute | solution.py:262
  255.7 25.3 %collective-permute-start.40 = (bf16[128,2048]{1,0:T(8,128)(2,1)}, bf16[128,2048]{1,0:T(8,128)(2,1)S(1)}, u32[]{:S(2)}, u32[]{:S(2)}) collective-permute-start(bf16[128,2048]{1,0:T(8,128)(2,1)} %copy-done.41), channel_id=1, source_target_pairs={{0,62},{2,0},{4,2},{6,4},{8,6},{10,8},{12,10},{14,12},{16,14},{18,... | collective-permute-start | bytes 1572872 | tf_op jit(solution)/shard_map/ppermute | solution.py:262
  290.9 28.0 %collective-permute-start.73 = (bf16[96,4096]{1,0:T(8,128)(2,1)}, bf16[96,4096]{1,0:T(8,128)(2,1)S(1)}, u32[]{:S(2)}, u32[]{:S(2)}) collective-permute-start(bf16[96,4096]{1,0:T(8,128)(2,1)} %get-tuple-element.75), channel_id=1, source_target_pairs={{0,1},{1,0},{2,3},{3,2},{4,5},{5,4},{6,7},{7,6},{8,9},{9,8},{10,11... | collective-permute-start | bytes 2359304 | tf_op jit(solution)/shard_map/ppermute | solution.py:265
  293.3 25.2 %collective-permute-start.26 = (bf16[128,2048]{1,0:T(8,128)(2,1)}, bf16[128,2048]{1,0:T(8,128)(2,1)S(1)}, u32[]{:S(2)}, u32[]{:S(2)}) collective-permute-start(bf16[128,2048]{1,0:T(8,128)(2,1)} %copy-done.44), channel_id=1, source_target_pairs={{0,2},{2,4},{4,6},{6,8},{8,10},{10,12},{12,14},{14,16},{16,18},{18... | collective-permute-start | bytes 1572872 | tf_op jit(solution)/shard_map/ppermute | solution.py:262
  293.3 25.2 %collective-permute-start.41 = (bf16[128,2048]{1,0:T(8,128)(2,1)}, bf16[128,2048]{1,0:T(8,128)(2,1)S(1)}, u32[]{:S(2)}, u32[]{:S(2)}) collective-permute-start(bf16[128,2048]{1,0:T(8,128)(2,1)} %copy-done.45), channel_id=1, source_target_pairs={{0,62},{2,0},{4,2},{6,4},{8,6},{10,8},{12,10},{14,12},{16,14},{18,... | collective-permute-start | bytes 1572872 | tf_op jit(solution)/shard_map/ppermute | solution.py:262
  328.3 28.0 %collective-permute-start.74 = (bf16[96,4096]{1,0:T(8,128)(2,1)}, bf16[96,4096]{1,0:T(8,128)(2,1)S(1)}, u32[]{:S(2)}, u32[]{:S(2)}) collective-permute-start(bf16[96,4096]{1,0:T(8,128)(2,1)} %get-tuple-element.78), channel_id=1, source_target_pairs={{0,1},{1,0},{2,3},{3,2},{4,5},{5,4},{6,7},{7,6},{8,9},{9,8},{10,11... | collective-permute-start | bytes 2359304 | tf_op jit(solution)/shard_map/ppermute | solution.py:265
  331.4 24.9 %collective-permute-start.27 = (bf16[128,2048]{1,0:T(8,128)(2,1)}, bf16[128,2048]{1,0:T(8,128)(2,1)S(1)}, u32[]{:S(2)}, u32[]{:S(2)}) collective-permute-start(bf16[128,2048]{1,0:T(8,128)(2,1)} %copy-done.48), channel_id=1, source_target_pairs={{0,2},{2,4},{4,6},{6,8},{8,10},{10,12},{12,14},{14,16},{16,18},{18... | collective-permute-start | bytes 1572872 | tf_op jit(solution)/shard_map/ppermute | solution.py:262
  331.5 24.8 %collective-permute-start.42 = (bf16[128,2048]{1,0:T(8,128)(2,1)}, bf16[128,2048]{1,0:T(8,128)(2,1)S(1)}, u32[]{:S(2)}, u32[]{:S(2)}) collective-permute-start(bf16[128,2048]{1,0:T(8,128)(2,1)} %copy-done.49), channel_id=1, source_target_pairs={{0,62},{2,0},{4,2},{6,4},{8,6},{10,8},{12,10},{14,12},{16,14},{18,... | collective-permute-start | bytes 1572872 | tf_op jit(solution)/shard_map/ppermute | solution.py:262
  366.1 28.1 %collective-permute-start.75 = (bf16[96,4096]{1,0:T(8,128)(2,1)}, bf16[96,4096]{1,0:T(8,128)(2,1)S(1)}, u32[]{:S(2)}, u32[]{:S(2)}) collective-permute-start(bf16[96,4096]{1,0:T(8,128)(2,1)} %get-tuple-element.81), channel_id=1, source_target_pairs={{0,1},{1,0},{2,3},{3,2},{4,5},{5,4},{6,7},{7,6},{8,9},{9,8},{10,11... | collective-permute-start | bytes 2359304 | tf_op jit(solution)/shard_map/ppermute | solution.py:265
  368.3 26.0 %collective-permute-start.28 = (bf16[128,2048]{1,0:T(8,128)(2,1)}, bf16[128,2048]{1,0:T(8,128)(2,1)S(1)}, u32[]{:S(2)}, u32[]{:S(2)}) collective-permute-start(bf16[128,2048]{1,0:T(8,128)(2,1)} %copy-done.52), channel_id=1, source_target_pairs={{0,2},{2,4},{4,6},{6,8},{8,10},{10,12},{12,14},{14,16},{16,18},{18... | collective-permute-start | bytes 1572872 | tf_op jit(solution)/shard_map/ppermute | solution.py:262
  368.4 25.9 %collective-permute-start.43 = (bf16[128,2048]{1,0:T(8,128)(2,1)}, bf16[128,2048]{1,0:T(8,128)(2,1)S(1)}, u32[]{:S(2)}, u32[]{:S(2)}) collective-permute-start(bf16[128,2048]{1,0:T(8,128)(2,1)} %copy-done.53), channel_id=1, source_target_pairs={{0,62},{2,0},{4,2},{6,4},{8,6},{10,8},{12,10},{14,12},{16,14},{18,... | collective-permute-start | bytes 1572872 | tf_op jit(solution)/shard_map/ppermute | solution.py:262
  404.1 26.9 %collective-permute-start.76 = (bf16[96,4096]{1,0:T(8,128)(2,1)}, bf16[96,4096]{1,0:T(8,128)(2,1)S(1)}, u32[]{:S(2)}, u32[]{:S(2)}) collective-permute-start(bf16[96,4096]{1,0:T(8,128)(2,1)} %get-tuple-element.84), channel_id=1, source_target_pairs={{0,1},{1,0},{2,3},{3,2},{4,5},{5,4},{6,7},{7,6},{8,9},{9,8},{10,11... | collective-permute-start | bytes 2359304 | tf_op jit(solution)/shard_map/ppermute | solution.py:265
  406.1 24.8 %collective-permute-start.29 = (bf16[128,2048]{1,0:T(8,128)(2,1)}, bf16[128,2048]{1,0:T(8,128)(2,1)S(1)}, u32[]{:S(2)}, u32[]{:S(2)}) collective-permute-start(bf16[128,2048]{1,0:T(8,128)(2,1)} %copy-done.56), channel_id=1, source_target_pairs={{0,2},{2,4},{4,6},{6,8},{8,10},{10,12},{12,14},{14,16},{16,18},{18... | collective-permute-start | bytes 1572872 | tf_op jit(solution)/shard_map/ppermute | solution.py:262
  406.2 24.8 %collective-permute-start.44 = (bf16[128,2048]{1,0:T(8,128)(2,1)}, bf16[128,2048]{1,0:T(8,128)(2,1)S(1)}, u32[]{:S(2)}, u32[]{:S(2)}) collective-permute-start(bf16[128,2048]{1,0:T(8,128)(2,1)} %copy-done.57), channel_id=1, source_target_pairs={{0,62},{2,0},{4,2},{6,4},{8,6},{10,8},{12,10},{14,12},{16,14},{18,... | collective-permute-start | bytes 1572872 | tf_op jit(solution)/shard_map/ppermute | solution.py:262
  440.8 28.5 %collective-permute-start.77 = (bf16[96,4096]{1,0:T(8,128)(2,1)}, bf16[96,4096]{1,0:T(8,128)(2,1)S(1)}, u32[]{:S(2)}, u32[]{:S(2)}) collective-permute-start(bf16[96,4096]{1,0:T(8,128)(2,1)} %get-tuple-element.87), channel_id=1, source_target_pairs={{0,1},{1,0},{2,3},{3,2},{4,5},{5,4},{6,7},{7,6},{8,9},{9,8},{10,11... | collective-permute-start | bytes 2359304 | tf_op jit(solution)/shard_map/ppermute | solution.py:265
  443.3 26.0 %collective-permute-start.30 = (bf16[128,2048]{1,0:T(8,128)(2,1)}, bf16[128,2048]{1,0:T(8,128)(2,1)S(1)}, u32[]{:S(2)}, u32[]{:S(2)}) collective-permute-start(bf16[128,2048]{1,0:T(8,128)(2,1)} %copy-done.60), channel_id=1, source_target_pairs={{0,2},{2,4},{4,6},{6,8},{8,10},{10,12},{12,14},{14,16},{16,18},{18... | collective-permute-start | bytes 1572872 | tf_op jit(solution)/shard_map/ppermute | solution.py:262
  443.4 25.9 %collective-permute-start.45 = (bf16[128,2048]{1,0:T(8,128)(2,1)}, bf16[128,2048]{1,0:T(8,128)(2,1)S(1)}, u32[]{:S(2)}, u32[]{:S(2)}) collective-permute-start(bf16[128,2048]{1,0:T(8,128)(2,1)} %copy-done.61), channel_id=1, source_target_pairs={{0,62},{2,0},{4,2},{6,4},{8,6},{10,8},{12,10},{14,12},{16,14},{18,... | collective-permute-start | bytes 1572872 | tf_op jit(solution)/shard_map/ppermute | solution.py:262
  479.1 26.9 %collective-permute-start.78 = (bf16[96,4096]{1,0:T(8,128)(2,1)}, bf16[96,4096]{1,0:T(8,128)(2,1)S(1)}, u32[]{:S(2)}, u32[]{:S(2)}) collective-permute-start(bf16[96,4096]{1,0:T(8,128)(2,1)} %get-tuple-element.90), channel_id=1, source_target_pairs={{0,1},{1,0},{2,3},{3,2},{4,5},{5,4},{6,7},{7,6},{8,9},{9,8},{10,11... | collective-permute-start | bytes 2359304 | tf_op jit(solution)/shard_map/ppermute | solution.py:265
  480.5 25.4 %collective-permute-start.31 = (bf16[128,2048]{1,0:T(8,128)(2,1)}, bf16[128,2048]{1,0:T(8,128)(2,1)S(1)}, u32[]{:S(2)}, u32[]{:S(2)}) collective-permute-start(bf16[128,2048]{1,0:T(8,128)(2,1)} %copy-done.64), channel_id=1, source_target_pairs={{0,2},{2,4},{4,6},{6,8},{8,10},{10,12},{12,14},{14,16},{16,18},{18... | collective-permute-start | bytes 1572872 | tf_op jit(solution)/shard_map/ppermute | solution.py:262
  480.5 25.4 %collective-permute-start.46 = (bf16[128,2048]{1,0:T(8,128)(2,1)}, bf16[128,2048]{1,0:T(8,128)(2,1)S(1)}, u32[]{:S(2)}, u32[]{:S(2)}) collective-permute-start(bf16[128,2048]{1,0:T(8,128)(2,1)} %copy-done.65), channel_id=1, source_target_pairs={{0,62},{2,0},{4,2},{6,4},{8,6},{10,8},{12,10},{14,12},{16,14},{18,... | collective-permute-start | bytes 1572872 | tf_op jit(solution)/shard_map/ppermute | solution.py:262
  515.8 28.2 %collective-permute-start.79 = (bf16[96,4096]{1,0:T(8,128)(2,1)}, bf16[96,4096]{1,0:T(8,128)(2,1)S(1)}, u32[]{:S(2)}, u32[]{:S(2)}) collective-permute-start(bf16[96,4096]{1,0:T(8,128)(2,1)} %get-tuple-element.93), channel_id=1, source_target_pairs={{0,1},{1,0},{2,3},{3,2},{4,5},{5,4},{6,7},{7,6},{8,9},{9,8},{10,11... | collective-permute-start | bytes 2359304 | tf_op jit(solution)/shard_map/ppermute | solution.py:265
  517.8 25.6 %collective-permute-start.32 = (bf16[128,2048]{1,0:T(8,128)(2,1)}, bf16[128,2048]{1,0:T(8,128)(2,1)S(1)}, u32[]{:S(2)}, u32[]{:S(2)}) collective-permute-start(bf16[128,2048]{1,0:T(8,128)(2,1)} %copy-done.68), channel_id=1, source_target_pairs={{0,2},{2,4},{4,6},{6,8},{8,10},{10,12},{12,14},{14,16},{16,18},{18... | collective-permute-start | bytes 1572872 | tf_op jit(solution)/shard_map/ppermute | solution.py:262
  518.3 25.1 %collective-permute-start.47 = (bf16[128,2048]{1,0:T(8,128)(2,1)}, bf16[128,2048]{1,0:T(8,128)(2,1)S(1)}, u32[]{:S(2)}, u32[]{:S(2)}) collective-permute-start(bf16[128,2048]{1,0:T(8,128)(2,1)} %copy-done.69), channel_id=1, source_target_pairs={{0,62},{2,0},{4,2},{6,4},{8,6},{10,8},{12,10},{14,12},{16,14},{18,... | collective-permute-start | bytes 1572872 | tf_op jit(solution)/shard_map/ppermute | solution.py:262
  (129 other events, 1100.2 us)

commit v3 on v2

--- a/solution.py
+++ b/solution.py
@@ -97,11 +97,10 @@
     if n_old and not fresh:
         take(1)
     (out_ref,) = take(1) if n_old else (None,)
-    keep_ref, give_ref = take(2) if n_src else (None, None)
-    step = 512
+    picked = take(2) if n_src else ()
     span = per_dev * WIN
     if n_old:
-        buf, in_sem, out_sem = refs
+        buf, was, in_sem, out_sem, was_sem = take(5)
         wide = out_ref.shape[2]
         spots = [(s, e) for s in range(n_old) for e in range(per_dev)]
 
@@ -110,20 +109,74 @@
             return out_ref.at[e, pl.ds(first, WIN), :]
 
         def fetch(sources):
-            for k, (s, e) in enumerate(spots):
-                if s in sources:
-                    pltpu.make_async_copy(window(s, e), buf.at[k], in_sem.at[k]).start()
-
-        def settle(sources):
-            for k, (s, e) in enumerate(spots):
-                if s in sources:
-                    pltpu.make_async_copy(buf.at[k], window(s, e), out_sem.at[k]).wait()
-
-        fetch((0, 1))
+            return [
+                pltpu.make_async_copy(window(s, e), buf.at[k], in_sem.at[k])
+                for k, (s, e) in enumerate(spots)
+                if s in sources
+            ]
+
+        def store(sources):
+            return [
+                pltpu.make_async_copy(buf.at[k], window(s, e), out_sem.at[k])
+                for k, (s, e) in enumerate(spots)
+                if s in sources
+            ]
+
+        def earlier(s):
+            rows = pl.ds(s * span, span)
+            return [
+                pltpu.make_async_copy(old.at[rows, :], was.at[i, rows, :], was_sem.at[2 * s + i])
+                for i, old in enumerate((keep_old, got_old))
+            ]
+
+    if n_src:
+        arrived = take(2 * n_src)
+        block, flow_sem, block_sem = take(3)
+        loads = [
+            pltpu.make_async_copy(flow, here, flow_sem.at[k])
+            for k, (flow, here) in enumerate(zip(flows, arrived))
+        ]
+        for load in loads:
+            load.start()
+    if n_old:
+        for copy in fetch((0, 1)):
+            copy.start()
+        for s in range(n_old):
+            for copy in earlier(s):
+                copy.start()
+    sent = []
+    for s in range(n_src):
+        for piece in range(2):
+            k = 2 * s + piece
+            loads[k].wait()
+            n, half = arrived[k].shape
+            spot = tabs[s][0, :, piece : piece + 1]
+            gate = tabs[s][0, :, 2:3]
+            row = lax.broadcasted_iota(jnp.int32, (2 * span, n), 1).astype(jnp.float32)
+            pick = (row == spot).astype(jnp.bfloat16)
+            acc = jnp.dot(pick, arrived[k][...], preferred_element_type=jnp.float32)
+            acc = (acc * gate).astype(jnp.bfloat16)
+            at = piece * half
+            for i in range(2):
+                block[i, s * span : (s + 1) * span, at : at + half] = acc[i * span : (i + 1) * span]
+        rows = pl.ds(s * span, span)
+        for i in range(2):
+            copy = pltpu.make_async_copy(
+                block.at[i, rows, :], picked[i].at[rows, :], block_sem.at[2 * s + i]
+            )
+            copy.start()
+            sent.append(copy)
+    if n_old:
+        step = wide // 2
         for k, (s, e) in enumerate(spots):
-            if s == 2 and e == 0:
-                settle((0, 1))
-                fetch((2,))
+            if e == 0:
+                if s == 2:
+                    for copy in store((0, 1)):
+                        copy.wait()
+                    for copy in fetch((2,)):
+                        copy.start()
+                for copy in earlier(s):
+                    copy.wait()
             pltpu.make_async_copy(window(s, e), buf.at[k], in_sem.at[k]).wait()
             shift = lax.rem(2 * CAP * sc_ref[n_src + s], 8)
             w = lax.broadcasted_iota(jnp.int32, (WIN, step), 0) - shift
@@ -132,34 +185,18 @@
             def merge(i, carry, k=k, mine=mine):
                 c = pl.multiple_of(i * step, step)
                 here = (pl.ds(k * WIN, WIN), pl.ds(c, step))
-                new = keep_old[here].astype(jnp.float32) + got_old[here].astype(jnp.float32)
+                new = was[0, here[0], here[1]].astype(jnp.float32)
+                new = new + was[1, here[0], here[1]].astype(jnp.float32)
                 old = buf[k, :, pl.ds(c, step)].astype(jnp.float32)
                 buf[k, :, pl.ds(c, step)] = jnp.where(mine, new, old).astype(buf.dtype)
                 return carry
 
             lax.fori_loop(0, wide // step, merge, 0)
             pltpu.make_async_copy(buf.at[k], window(s, e), out_sem.at[k]).start()
-    for s in range(n_src):
-        for piece in range(2):
-            flow = flows[2 * s + piece]
-            n, half = flow.shape
-            spot = tabs[s][0, :, piece : piece + 1]
-            gate = tabs[s][0, :, 2:3]
-            row = lax.broadcasted_iota(jnp.int32, (2 * span, n), 1).astype(jnp.float32)
-            pick = (row == spot).astype(jnp.bfloat16)
-
-            def column(i, carry, s=s, piece=piece, flow=flow, pick=pick, gate=gate, half=half):
-                c = pl.multiple_of(i * step, step)
-                acc = jnp.dot(pick, flow[:, pl.ds(c, step)], preferred_element_type=jnp.float32)
-                acc = (acc * gate).astype(jnp.bfloat16)
-                at = pl.multiple_of(piece * half + i * step, step)
-                keep_ref[s * span : (s + 1) * span, pl.ds(at, step)] = acc[:span]
-                give_ref[s * span : (s + 1) * span, pl.ds(at, step)] = acc[span:]
-                return carry
-
-            lax.fori_loop(0, half // step, column, 0)
-    if n_old:
-        settle((2,) if n_old > 2 else (0, 1))
+        for copy in store((2,) if n_old > 2 else (0, 1)):
+            copy.wait()
+    for copy in sent:
+        copy.wait()
 
 
 def place(out, table, sources, flows, old, shape, per_dev):
@@ -169,7 +206,6 @@
     span = per_dev * WIN
     width = shape.shape[2]
     scalars = jnp.stack([*sources, *(old[0] if old else ())]).astype(jnp.int32)
-    flat = lambda a: pl.BlockSpec(a.shape, lambda i, sc: (0, 0))
     anywhere = pl.BlockSpec(memory_space=pl.ANY)
     args, specs, outs, out_specs, scratch, alias = [], [], [], [], [], {}
     for s in range(n_src):
@@ -177,7 +213,7 @@
         specs.append(pl.BlockSpec((1, *table.shape[1:]), lambda i, sc, s=s: (sc[s], 0, 0)))
     for a in (*flows, *(old[1:] if old else ())):
         args.append(a)
-        specs.append(flat(a))
+        specs.append(anywhere)
     if n_old:
         if not fresh:
             alias = {1 + len(args): 0}
@@ -188,13 +224,21 @@
         count = n_old * per_dev
         scratch = [
             pltpu.VMEM((count, WIN, width), shape.dtype),
+            pltpu.VMEM((2, n_old * span, width), shape.dtype),
             pltpu.SemaphoreType.DMA((count,)),
             pltpu.SemaphoreType.DMA((count,)),
+            pltpu.SemaphoreType.DMA((2 * n_old,)),
         ]
     if n_src:
         block = jax.ShapeDtypeStruct((n_src * span, width), shape.dtype)
         outs += [block, block]
-        out_specs += [flat(block), flat(block)]
+        out_specs += [anywhere, anywhere]
+        scratch += [
+            *(pltpu.VMEM(a.shape, a.dtype) for a in flows),
+            pltpu.VMEM((2, n_src * span, width), shape.dtype),
+            pltpu.SemaphoreType.DMA((2 * n_src,)),
+            pltpu.SemaphoreType.DMA((2 * n_src,)),
+        ]
     result = pl.pallas_call(
         functools.partial(place_body, n_src, n_old, fresh, per_dev),
         grid_spec=pltpu.PrefetchScalarGridSpec(
@@ -221,7 +265,7 @@
     )(scalar, *arrays)
 
 
-def trade(message, totals, chips):
+def trade(message, totals, chips, arrivals):
     z = lax.axis_index("chip")
     lanes = message.shape[-1]
     data = message
@@ -234,6 +278,7 @@
         rows = chips // 2
         packed = jnp.concatenate([give.reshape(rows, lanes), totals], axis=0)
         got = lax.ppermute(packed, "chip", [(i, i ^ (1 << step)) for i in range(chips)])
+        got, _ = lax.optimization_barrier((got, arrivals[step]))
         totals = totals + got[rows:]
         came = got[:rows].reshape(blocks // 2, seen, lanes)
         low = jnp.where(mine == 0, keep, came)
@@ -277,6 +322,19 @@
         functools.partial(order_body, chips, per_chip), zs,
         (expert_ids, ids_t, tokens), [sds((local_rows, half), tokens.dtype)] * 4,
     )
+    fars = (reach, reach - 1, reach - 1, reach)
+    ways = (onward, onward, backward, backward)
+    own, hops = flows[:2], []
+    for h in range(1, reach + 1):
+        sent = []
+        for x, far, way in zip(flows, fars, ways):
+            if h <= far:
+                x = send(x[: need(h, far)], way)
+                sent.append(x)
+            else:
+                sent.append(None)
+        flows = sent
+        hops.append([x for x in flows if x is not None])
     (table,) = whole_call(
         functools.partial(route_body, chips, per_chip), zs,
         (expert_ids, ids_t, tokens, router_weight), [sds((32, EXPERTS), jnp.float32)],
@@ -285,7 +343,9 @@
     message = table[:rows].reshape(rows, chips, per_chip).transpose(1, 2, 0)
     message = message.reshape(chips, per_chip * rows)
     message = jnp.pad(message, ((0, 0), (0, 128 - per_chip * rows)))
-    got, totals = trade(message, table[rows : rows + 2], chips)
+    got, totals = trade(
+        message, table[rows : rows + 2], chips, [arrived[2] for arrived in hops[: reach - 1]]
+    )
     token_total = jnp.float32(local_rows * 2 * chips)
     loss = EXPERTS * jnp.sum(totals[0] * totals[1]) / (token_total * token_total * TOP_K)
 
@@ -315,22 +375,12 @@
     windows = jnp.pad(windows, ((0, 0), (0, 0), (0, 5)))
 
     shape = sds((per_dev, 2 * chips * CAP, width), tokens.dtype)
-    out, (keep, give) = place(None, windows, [z], flows[:2], None, shape, per_dev)
+    out, (keep, give) = place(None, windows, [z], own, None, shape, per_dev)
     old = ([z], keep, swap(give))
-    fars = (reach, reach - 1, reach - 1, reach)
-    ways = (onward, onward, backward, backward)
     live, sources = [], []
-    for h in range(1, reach + 1):
+    for h, arrived in enumerate(hops, 1):
         up, down = (z - h) % chips, (z + h) % chips
-        sent = []
-        for x, far, way in zip(flows, fars, ways):
-            if h <= far:
-                x = send(x[: need(h, far)], way)
-                sent.append(x)
-            else:
-                sent.append(None)
-        flows = sent
-        live += [x for x in flows if x is not None]
+        live += arrived
         sources += [up, down] if h < reach else [up]
         if h == reach - 1:
             continue

time: 640 us -> 609 us (0.952)
  Pallas kernels: 143 us -> 92.1 us
  waiting for transfers between devices: 280 us -> 313 us
  starting transfers between devices: 156 us -> 144 us
    pallas_call x17, Pallas kernels: 136 us -> 86 us  [place(): pl.pallas_call(functools.partial(place_body, n_src, n_old, fresh, per_dev...]
    ppermute x5, starting transfers between devices: 50.6 us -> 12.3 us  [trade(): lax.ppermute(packed, 'chip', [(i, i ^ 1 << step) for i in range(chips)])]
    ppermute x62, starting transfers between devices: 73.9 us -> 106 us  [send(): return lax.ppermute(x, 'chip', to)]
    ppermute x5, waiting for transfers between devices: 4.39 us -> 28.9 us  [trade(): lax.ppermute(packed, 'chip', [(i, i ^ 1 << step) for i in range(chips)])]
    ppermute x62, waiting for transfers between devices: 273 us -> 281 us  [send(): return lax.ppermute(x, 'chip', to)]
    unnamed x157 -> x143, local copies, waits for them, and re-layouts: 20.8 us -> 19.6 us
  transfers between devices with their start and end apart: 84 -> 84, of which waited for: 41 -> 45; matrix products, arithmetic and copies ran while one was open for 4% -> 5% of each run, Pallas kernels for 1% -> 1%
where the time goes in v3:
time: 609 us; the launch traced here: 599 us
  waiting for transfers between devices  313 us (51%)
  starting transfers between devices  144 us (24%)
  Pallas kernels  92.1 us (15%)
  local copies, waits for them, and re-layouts  35.2 us (6%)
  other arithmetic  11.5 us (2%)
    ppermute x62, waiting for transfers between devices, send(): return lax.ppermute(x, 'chip', to)  281 us
    ppermute x62, starting transfers between devices, send(): return lax.ppermute(x, 'chip', to)  106 us
    pallas_call x17, Pallas kernels, place(): pl.pallas_call(functools.partial(place_body, n_src, n_old, fresh, per_dev...  86 us
    ppermute x5, waiting for transfers between devices, trade(): lax.ppermute(packed, 'chip', [(i, i ^ 1 << step) for i in range(chips)])  28.9 us
    ppermute x16, starting transfers between devices, swap(): return lax.ppermute(x, 'core', [(0, 1), (1, 0)])  25.5 us
    unnamed x143, local copies, waits for them, and re-layouts  19.6 us
    ppermute x5, starting transfers between devices, trade(): lax.ppermute(packed, 'chip', [(i, i ^ 1 << step) for i in range(chips)])  12.3 us
  transfers between devices with their start and end apart: 84, of which 45 were waited for; matrix products, arithmetic and copies ran while one was open for 5% of the time, Pallas kernels for 1%

profile of v3, /device:TPU:37, one launch (start us, length us, event | category | flops | bytes accessed | tf_op | source)
XLA Modules:
  0.0 599.3 jit_solution(6723692363893806084)
XLA Ops:
  5.1 23.6 %collective-permute-start.1 = (bf16[128,2048]{1,0:T(8,128)(2,1)}, bf16[128,2048]{1,0:T(8,128)(2,1)S(1)}, u32[]{:S(2)}, u32[]{:S(2)}) collective-permute-start(bf16[128,2048]{1,0:T(8,128)(2,1)} %get-tuple-element.58), channel_id=1, source_target_pairs={{0,62},{2,0},{4,2},{6,4},{8,6},{10,8},{12,10},{14,12},{16,14},{18,... | collective-permute-start | bytes 1572872 | tf_op jit(solution)/shard_map/ppermute | solution.py:307
  56.7 6.5 %collective-permute-done.4 = f32[18,128]{1,0:T(8,128)S(1)} collective-permute-done((f32[18,128]{1,0:T(8,128)S(1)}, f32[18,128]{1,0:T(8,128)S(1)}, u32[]{:S(2)}, u32[]{:S(2)}) %collective-permute-start.4) | collective-permute-done | bytes 9248 | tf_op jit(solution)/shard_map/ppermute | solution.py:280
  69.2 11.3 %collective-permute-done.6 = f32[18,128]{1,0:T(8,128)S(1)} collective-permute-done((f32[18,128]{1,0:T(8,128)S(1)}, f32[18,128]{1,0:T(8,128)S(1)}, u32[]{:S(2)}, u32[]{:S(2)}) %collective-permute-start.6) | collective-permute-done | bytes 9248 | tf_op jit(solution)/shard_map/ppermute | solution.py:280
  80.7 11.9 %collective-permute-start.8 = (f32[18,128]{1,0:T(8,128)S(1)}, f32[18,128]{1,0:T(8,128)S(1)}, u32[]{:S(2)}, u32[]{:S(2)}) collective-permute-start(f32[18,128]{1,0:T(8,128)S(1)} %pad_maximum_fusion.9), channel_id=1, source_target_pairs={{0,32},{2,34},{4,36},{6,38},{8,40},{10,42},{12,44},{14,46},{16,48}... | collective-permute-start | bytes 27656 | tf_op jit(solution)/shard_map/ppermute | solution.py:280
  111.1 6.3 %collective-permute-start.67 = (bf16[48,4096]{1,0:T(8,128)(2,1)}, bf16[48,4096]{1,0:T(8,128)(2,1)S(1)}, u32[]{:S(2)}, u32[]{:S(2)}) collective-permute-start(bf16[48,4096]{1,0:T(8,128)(2,1)} %get-tuple-element.68), channel_id=1, source_target_pairs={{0,1},{1,0},{2,3},{3,2},{4,5},{5,4},{6,7},{7,6},{8,9},{9,8},{10,11... | collective-permute-start | bytes 1179656 | tf_op jit(solution)/shard_map/ppermute | solution.py:310
  135.5 8.2 %collective-permute-done.11.refs_2_ = bf16[128,2048]{1,0:T(8,128)(2,1)S(1)} collective-permute-done((bf16[128,2048]{1,0:T(8,128)(2,1)}, bf16[128,2048]{1,0:T(8,128)(2,1)S(1)}, u32[]{:S(2)}, u32[]{:S(2)}) %collective-permute-start.11) | collective-permute-done | bytes 524320 | tf_op jit(solution)/shard_map/ppermute | solution.py:307
  143.7 11.2 %collective-permute-done.26.refs_3_ = bf16[128,2048]{1,0:T(8,128)(2,1)} collective-permute-done((bf16[128,2048]{1,0:T(8,128)(2,1)}, bf16[128,2048]{1,0:T(8,128)(2,1)}, u32[]{:S(2)}, u32[]{:S(2)}) %collective-permute-start.26) | collective-permute-done | bytes 524320 | tf_op jit(solution)/shard_map/ppermute | solution.py:307
  167.7 9.3 %collective-permute-done.12.refs_2_ = bf16[128,2048]{1,0:T(8,128)(2,1)S(1)} collective-permute-done((bf16[128,2048]{1,0:T(8,128)(2,1)}, bf16[128,2048]{1,0:T(8,128)(2,1)S(1)}, u32[]{:S(2)}, u32[]{:S(2)}) %collective-permute-start.12) | collective-permute-done | bytes 524320 | tf_op jit(solution)/shard_map/ppermute | solution.py:307
  176.9 11.2 %collective-permute-done.27.refs_3_ = bf16[128,2048]{1,0:T(8,128)(2,1)S(1)} collective-permute-done((bf16[128,2048]{1,0:T(8,128)(2,1)}, bf16[128,2048]{1,0:T(8,128)(2,1)S(1)}, u32[]{:S(2)}, u32[]{:S(2)}) %collective-permute-start.27) | collective-permute-done | bytes 524320 | tf_op jit(solution)/shard_map/ppermute | solution.py:307
  200.3 10.5 %collective-permute-done.13.refs_2_ = bf16[128,2048]{1,0:T(8,128)(2,1)S(1)} collective-permute-done((bf16[128,2048]{1,0:T(8,128)(2,1)}, bf16[128,2048]{1,0:T(8,128)(2,1)S(1)}, u32[]{:S(2)}, u32[]{:S(2)}) %collective-permute-start.13) | collective-permute-done | bytes 524320 | tf_op jit(solution)/shard_map/ppermute | solution.py:307
  210.8 11.2 %collective-permute-done.28.refs_3_ = bf16[128,2048]{1,0:T(8,128)(2,1)S(1)} collective-permute-done((bf16[128,2048]{1,0:T(8,128)(2,1)}, bf16[128,2048]{1,0:T(8,128)(2,1)S(1)}, u32[]{:S(2)}, u32[]{:S(2)}) %collective-permute-start.28) | collective-permute-done | bytes 524320 | tf_op jit(solution)/shard_map/ppermute | solution.py:307
  223.3 5.2 place.21
  233.0 11.4 %collective-permute-done.14.refs_2_ = bf16[128,2048]{1,0:T(8,128)(2,1)S(1)} collective-permute-done((bf16[128,2048]{1,0:T(8,128)(2,1)}, bf16[128,2048]{1,0:T(8,128)(2,1)S(1)}, u32[]{:S(2)}, u32[]{:S(2)}) %collective-permute-start.14) | collective-permute-done | bytes 524320 | tf_op jit(solution)/shard_map/ppermute | solution.py:307
  244.4 11.3 %collective-permute-done.29.refs_3_ = bf16[128,2048]{1,0:T(8,128)(2,1)} collective-permute-done((bf16[128,2048]{1,0:T(8,128)(2,1)}, bf16[128,2048]{1,0:T(8,128)(2,1)}, u32[]{:S(2)}, u32[]{:S(2)}) %collective-permute-start.29) | collective-permute-done | bytes 524320 | tf_op jit(solution)/shard_map/ppermute | solution.py:307
  267.9 8.6 %collective-permute-done.40.refs_4_ = bf16[128,2048]{1,0:T(8,128)(2,1)S(1)} collective-permute-done((bf16[128,2048]{1,0:T(8,128)(2,1)S(1)}, bf16[128,2048]{1,0:T(8,128)(2,1)S(1)}, u32[]{:S(2)}, u32[]{:S(2)}) %collective-permute-start.40) | collective-permute-done | bytes 524320 | tf_op jit(solution)/shard_map/ppermute | solution.py:307
  277.8 11.2 %collective-permute-done.30.refs_3_ = bf16[128,2048]{1,0:T(8,128)(2,1)S(1)} collective-permute-done((bf16[128,2048]{1,0:T(8,128)(2,1)}, bf16[128,2048]{1,0:T(8,128)(2,1)S(1)}, u32[]{:S(2)}, u32[]{:S(2)}) %collective-permute-start.30) | collective-permute-done | bytes 524320 | tf_op jit(solution)/shard_map/ppermute | solution.py:307
  301.6 8.9 %collective-permute-done.41.refs_4_ = bf16[128,2048]{1,0:T(8,128)(2,1)S(1)} collective-permute-done((bf16[128,2048]{1,0:T(8,128)(2,1)}, bf16[128,2048]{1,0:T(8,128)(2,1)S(1)}, u32[]{:S(2)}, u32[]{:S(2)}) %collective-permute-start.41) | collective-permute-done | bytes 524320 | tf_op jit(solution)/shard_map/ppermute | solution.py:307
  311.8 11.2 %collective-permute-done.31.refs_3_ = bf16[128,2048]{1,0:T(8,128)(2,1)S(1)} collective-permute-done((bf16[128,2048]{1,0:T(8,128)(2,1)}, bf16[128,2048]{1,0:T(8,128)(2,1)S(1)}, u32[]{:S(2)}, u32[]{:S(2)}) %collective-permute-start.31) | collective-permute-done | bytes 524320 | tf_op jit(solution)/shard_map/ppermute | solution.py:307
  335.4 8.8 %collective-permute-done.42.refs_4_ = bf16[128,2048]{1,0:T(8,128)(2,1)S(1)} collective-permute-done((bf16[128,2048]{1,0:T(8,128)(2,1)}, bf16[128,2048]{1,0:T(8,128)(2,1)S(1)}, u32[]{:S(2)}, u32[]{:S(2)}) %collective-permute-start.42) | collective-permute-done | bytes 524320 | tf_op jit(solution)/shard_map/ppermute | solution.py:307
  345.2 11.2 %collective-permute-done.32.refs_3_ = bf16[128,2048]{1,0:T(8,128)(2,1)S(1)} collective-permute-done((bf16[128,2048]{1,0:T(8,128)(2,1)}, bf16[128,2048]{1,0:T(8,128)(2,1)S(1)}, u32[]{:S(2)}, u32[]{:S(2)}) %collective-permute-start.32) | collective-permute-done | bytes 524320 | tf_op jit(solution)/shard_map/ppermute | solution.py:307
  369.3 8.4 %collective-permute-done.43.refs_4_ = bf16[128,2048]{1,0:T(8,128)(2,1)S(1)} collective-permute-done((bf16[128,2048]{1,0:T(8,128)(2,1)}, bf16[128,2048]{1,0:T(8,128)(2,1)S(1)}, u32[]{:S(2)}, u32[]{:S(2)}) %collective-permute-start.43) | collective-permute-done | bytes 524320 | tf_op jit(solution)/shard_map/ppermute | solution.py:307
  378.8 11.2 %collective-permute-done.33.refs_3_ = bf16[128,2048]{1,0:T(8,128)(2,1)S(1)} collective-permute-done((bf16[128,2048]{1,0:T(8,128)(2,1)}, bf16[128,2048]{1,0:T(8,128)(2,1)S(1)}, u32[]{:S(2)}, u32[]{:S(2)}) %collective-permute-start.33) | collective-permute-done | bytes 524320 | tf_op jit(solution)/shard_map/ppermute | solution.py:307
  402.5 8.8 %collective-permute-done.44.refs_4_ = bf16[128,2048]{1,0:T(8,128)(2,1)S(1)} collective-permute-done((bf16[128,2048]{1,0:T(8,128)(2,1)}, bf16[128,2048]{1,0:T(8,128)(2,1)S(1)}, u32[]{:S(2)}, u32[]{:S(2)}) %collective-permute-start.44) | collective-permute-done | bytes 524320 | tf_op jit(solution)/shard_map/ppermute | solution.py:307
  412.4 11.2 %collective-permute-done.34.refs_3_ = bf16[128,2048]{1,0:T(8,128)(2,1)S(1)} collective-permute-done((bf16[128,2048]{1,0:T(8,128)(2,1)}, bf16[128,2048]{1,0:T(8,128)(2,1)S(1)}, u32[]{:S(2)}, u32[]{:S(2)}) %collective-permute-start.34) | collective-permute-done | bytes 524320 | tf_op jit(solution)/shard_map/ppermute | solution.py:307
  436.1 8.8 %collective-permute-done.45.refs_4_ = bf16[128,2048]{1,0:T(8,128)(2,1)S(1)} collective-permute-done((bf16[128,2048]{1,0:T(8,128)(2,1)}, bf16[128,2048]{1,0:T(8,128)(2,1)S(1)}, u32[]{:S(2)}, u32[]{:S(2)}) %collective-permute-start.45) | collective-permute-done | bytes 524320 | tf_op jit(solution)/shard_map/ppermute | solution.py:307
  445.9 11.2 %collective-permute-done.35.refs_3_ = bf16[128,2048]{1,0:T(8,128)(2,1)S(1)} collective-permute-done((bf16[128,2048]{1,0:T(8,128)(2,1)}, bf16[128,2048]{1,0:T(8,128)(2,1)S(1)}, u32[]{:S(2)}, u32[]{:S(2)}) %collective-permute-start.35) | collective-permute-done | bytes 524320 | tf_op jit(solution)/shard_map/ppermute | solution.py:307
  469.7 8.9 %collective-permute-done.46.refs_4_ = bf16[128,2048]{1,0:T(8,128)(2,1)S(1)} collective-permute-done((bf16[128,2048]{1,0:T(8,128)(2,1)}, bf16[128,2048]{1,0:T(8,128)(2,1)S(1)}, u32[]{:S(2)}, u32[]{:S(2)}) %collective-permute-start.46) | collective-permute-done | bytes 524320 | tf_op jit(solution)/shard_map/ppermute | solution.py:307
  480.0 11.2 %collective-permute-done.36.refs_3_ = bf16[128,2048]{1,0:T(8,128)(2,1)} collective-permute-done((bf16[128,2048]{1,0:T(8,128)(2,1)}, bf16[128,2048]{1,0:T(8,128)(2,1)}, u32[]{:S(2)}, u32[]{:S(2)}) %collective-permute-start.36) | collective-permute-done | bytes 524320 | tf_op jit(solution)/shard_map/ppermute | solution.py:307
  503.1 8.8 %collective-permute-done.47.refs_4_ = bf16[128,2048]{1,0:T(8,128)(2,1)S(1)} collective-permute-done((bf16[128,2048]{1,0:T(8,128)(2,1)}, bf16[128,2048]{1,0:T(8,128)(2,1)S(1)}, u32[]{:S(2)}, u32[]{:S(2)}) %collective-permute-start.47) | collective-permute-done | bytes 524320 | tf_op jit(solution)/shard_map/ppermute | solution.py:307
  513.0 11.2 %collective-permute-done.37.refs_3_ = bf16[128,2048]{1,0:T(8,128)(2,1)S(1)} collective-permute-done((bf16[128,2048]{1,0:T(8,128)(2,1)}, bf16[128,2048]{1,0:T(8,128)(2,1)S(1)}, u32[]{:S(2)}, u32[]{:S(2)}) %collective-permute-start.37) | collective-permute-done | bytes 524320 | tf_op jit(solution)/shard_map/ppermute | solution.py:307
  542.0 10.8 %collective-permute-done.48.refs_4_ = bf16[72,2048]{1,0:T(8,128)(2,1)S(1)} collective-permute-done((bf16[72,2048]{1,0:T(8,128)(2,1)S(1)}, bf16[72,2048]{1,0:T(8,128)(2,1)S(1)}, u32[]{:S(2)}, u32[]{:S(2)}) %collective-permute-start.48) | collective-permute-done | bytes 294944 | tf_op jit(solution)/shard_map/ppermute | solution.py:307
  581.0 5.7 place.32
  (373 shorter events, 270.2 us)
Async XLA Ops:
  5.1 34.6 %collective-permute-start.1 = (bf16[128,2048]{1,0:T(8,128)(2,1)}, bf16[128,2048]{1,0:T(8,128)(2,1)S(1)}, u32[]{:S(2)}, u32[]{:S(2)}) collective-permute-start(bf16[128,2048]{1,0:T(8,128)(2,1)} %get-tuple-element.58), channel_id=1, source_target_pairs={{0,62},{2,0},{4,2},{6,4},{8,6},{10,8},{12,10},{14,12},{16,14},{18,... | collective-permute-start | bytes 1572872 | tf_op jit(solution)/shard_map/ppermute | solution.py:307
  92.6 25.4 %collective-permute-start.10 = (bf16[128,2048]{1,0:T(8,128)(2,1)}, bf16[128,2048]{1,0:T(8,128)(2,1)}, u32[]{:S(2)}, u32[]{:S(2)}) collective-permute-start(bf16[128,2048]{1,0:T(8,128)(2,1)} %get-tuple-element.64.refs_1_), channel_id=1, source_target_pairs={{0,2},{2,4},{4,6},{6,8},{8,10},{10,12},{12,14},{14,16},{16,18},{18... | collective-permute-start | bytes 1572872 | tf_op jit(solution)/shard_map/ppermute | solution.py:307
  124.6 30.3 %collective-permute-start.68 = (bf16[96,4096]{1,0:T(8,128)(2,1)}, bf16[96,4096]{1,0:T(8,128)(2,1)S(1)}, u32[]{:S(2)}, u32[]{:S(2)}) collective-permute-start(bf16[96,4096]{1,0:T(8,128)(2,1)} %get-tuple-element.70), channel_id=1, source_target_pairs={{0,1},{1,0},{2,3},{3,2},{4,5},{5,4},{6,7},{7,6},{8,9},{9,8},{10,11... | collective-permute-start | bytes 2359304 | tf_op jit(solution)/shard_map/ppermute | solution.py:310
  161.0 27.1 %collective-permute-start.69 = (bf16[96,4096]{1,0:T(8,128)(2,1)}, bf16[96,4096]{1,0:T(8,128)(2,1)S(1)}, u32[]{:S(2)}, u32[]{:S(2)}) collective-permute-start(bf16[96,4096]{1,0:T(8,128)(2,1)} %get-tuple-element.73), channel_id=1, source_target_pairs={{0,1},{1,0},{2,3},{3,2},{4,5},{5,4},{6,7},{7,6},{8,9},{9,8},{10,11... | collective-permute-start | bytes 2359304 | tf_op jit(solution)/shard_map/ppermute | solution.py:310
  194.6 27.5 %collective-permute-start.70 = (bf16[96,4096]{1,0:T(8,128)(2,1)}, bf16[96,4096]{1,0:T(8,128)(2,1)S(1)}, u32[]{:S(2)}, u32[]{:S(2)}) collective-permute-start(bf16[96,4096]{1,0:T(8,128)(2,1)} %get-tuple-element.76), channel_id=1, source_target_pairs={{0,1},{1,0},{2,3},{3,2},{4,5},{5,4},{6,7},{7,6},{8,9},{9,8},{10,11... | collective-permute-start | bytes 2359304 | tf_op jit(solution)/shard_map/ppermute | solution.py:310
  197.1 25.0 %collective-permute-start.28 = (bf16[128,2048]{1,0:T(8,128)(2,1)}, bf16[128,2048]{1,0:T(8,128)(2,1)S(1)}, u32[]{:S(2)}, u32[]{:S(2)}) collective-permute-start(bf16[128,2048]{1,0:T(8,128)(2,1)} %copy-done.60), channel_id=1, source_target_pairs={{0,2},{2,4},{4,6},{6,8},{8,10},{10,12},{12,14},{14,16},{16,18},{18... | collective-permute-start | bytes 1572872 | tf_op jit(solution)/shard_map/ppermute | solution.py:307
  197.2 24.9 %collective-permute-start.53 = (bf16[128,2048]{1,0:T(8,128)(2,1)}, bf16[128,2048]{1,0:T(8,128)(2,1)S(1)}, u32[]{:S(2)}, u32[]{:S(2)}) collective-permute-start(bf16[128,2048]{1,0:T(8,128)(2,1)} %copy-done.61), channel_id=1, source_target_pairs={{0,62},{2,0},{4,2},{6,4},{8,6},{10,8},{12,10},{14,12},{16,14},{18,... | collective-permute-start | bytes 1572872 | tf_op jit(solution)/shard_map/ppermute | solution.py:307
  228.5 27.2 %collective-permute-start.71 = (bf16[96,4096]{1,0:T(8,128)(2,1)}, bf16[96,4096]{1,0:T(8,128)(2,1)S(1)}, u32[]{:S(2)}, u32[]{:S(2)}) collective-permute-start(bf16[96,4096]{1,0:T(8,128)(2,1)} %get-tuple-element.79), channel_id=1, source_target_pairs={{0,1},{1,0},{2,3},{3,2},{4,5},{5,4},{6,7},{7,6},{8,9},{9,8},{10,11... | collective-permute-start | bytes 2359304 | tf_op jit(solution)/shard_map/ppermute | solution.py:310
  229.7 26.1 %collective-permute-start.29 = (bf16[128,2048]{1,0:T(8,128)(2,1)}, bf16[128,2048]{1,0:T(8,128)(2,1)}, u32[]{:S(2)}, u32[]{:S(2)}) collective-permute-start(bf16[128,2048]{1,0:T(8,128)(2,1)} %copy-done.63), channel_id=1, source_target_pairs={{0,2},{2,4},{4,6},{6,8},{8,10},{10,12},{12,14},{14,16},{16,18},{18... | collective-permute-start | bytes 1572872 | tf_op jit(solution)/shard_map/ppermute | solution.py:307
  229.7 26.1 %collective-permute-start.54 = (bf16[128,2048]{1,0:T(8,128)(2,1)}, bf16[128,2048]{1,0:T(8,128)(2,1)S(1)}, u32[]{:S(2)}, u32[]{:S(2)}) collective-permute-start(bf16[128,2048]{1,0:T(8,128)(2,1)} %copy-done.64), channel_id=1, source_target_pairs={{0,62},{2,0},{4,2},{6,4},{8,6},{10,8},{12,10},{14,12},{16,14},{18,... | collective-permute-start | bytes 1572872 | tf_op jit(solution)/shard_map/ppermute | solution.py:307
  262.0 27.0 %collective-permute-start.72 = (bf16[96,4096]{1,0:T(8,128)(2,1)}, bf16[96,4096]{1,0:T(8,128)(2,1)S(1)}, u32[]{:S(2)}, u32[]{:S(2)}) collective-permute-start(bf16[96,4096]{1,0:T(8,128)(2,1)} %get-tuple-element.82), channel_id=1, source_target_pairs={{0,1},{1,0},{2,3},{3,2},{4,5},{5,4},{6,7},{7,6},{8,9},{9,8},{10,11... | collective-permute-start | bytes 2359304 | tf_op jit(solution)/shard_map/ppermute | solution.py:310
  264.6 24.4 %collective-permute-start.30 = (bf16[128,2048]{1,0:T(8,128)(2,1)}, bf16[128,2048]{1,0:T(8,128)(2,1)S(1)}, u32[]{:S(2)}, u32[]{:S(2)}) collective-permute-start(bf16[128,2048]{1,0:T(8,128)(2,1)} %collective-permute-done.29.refs_3_), channel_id=1, source_target_pairs={{0,2},{2,4},{4,6},{6,8},{8,10},{10,12},{12,14},{14,16},{16,18},{18... | collective-permute-start | bytes 1572872 | tf_op jit(solution)/shard_map/ppermute | solution.py:307
  264.7 24.4 %collective-permute-start.55 = (bf16[128,2048]{1,0:T(8,128)(2,1)}, bf16[128,2048]{1,0:T(8,128)(2,1)S(1)}, u32[]{:S(2)}, u32[]{:S(2)}) collective-permute-start(bf16[128,2048]{1,0:T(8,128)(2,1)} %copy-done.57), channel_id=1, source_target_pairs={{0,62},{2,0},{4,2},{6,4},{8,6},{10,8},{12,10},{14,12},{16,14},{18,... | collective-permute-start | bytes 1572872 | tf_op jit(solution)/shard_map/ppermute | solution.py:307
  295.5 27.6 %collective-permute-start.73 = (bf16[96,4096]{1,0:T(8,128)(2,1)}, bf16[96,4096]{1,0:T(8,128)(2,1)S(1)}, u32[]{:S(2)}, u32[]{:S(2)}) collective-permute-start(bf16[96,4096]{1,0:T(8,128)(2,1)} %get-tuple-element.85), channel_id=1, source_target_pairs={{0,1},{1,0},{2,3},{3,2},{4,5},{5,4},{6,7},{7,6},{8,9},{9,8},{10,11... | collective-permute-start | bytes 2359304 | tf_op jit(solution)/shard_map/ppermute | solution.py:310
  298.4 24.7 %collective-permute-start.31 = (bf16[128,2048]{1,0:T(8,128)(2,1)}, bf16[128,2048]{1,0:T(8,128)(2,1)S(1)}, u32[]{:S(2)}, u32[]{:S(2)}) collective-permute-start(bf16[128,2048]{1,0:T(8,128)(2,1)} %copy-done.33), channel_id=1, source_target_pairs={{0,2},{2,4},{4,6},{6,8},{8,10},{10,12},{12,14},{14,16},{16,18},{18... | collective-permute-start | bytes 1572872 | tf_op jit(solution)/shard_map/ppermute | solution.py:307
  298.6 24.4 %collective-permute-start.56 = (bf16[128,2048]{1,0:T(8,128)(2,1)}, bf16[128,2048]{1,0:T(8,128)(2,1)S(1)}, u32[]{:S(2)}, u32[]{:S(2)}) collective-permute-start(bf16[128,2048]{1,0:T(8,128)(2,1)} %copy-done.34), channel_id=1, source_target_pairs={{0,62},{2,0},{4,2},{6,4},{8,6},{10,8},{12,10},{14,12},{16,14},{18,... | collective-permute-start | bytes 1572872 | tf_op jit(solution)/shard_map/ppermute | solution.py:307
  329.5 27.0 %collective-permute-start.74 = (bf16[96,4096]{1,0:T(8,128)(2,1)}, bf16[96,4096]{1,0:T(8,128)(2,1)S(1)}, u32[]{:S(2)}, u32[]{:S(2)}) collective-permute-start(bf16[96,4096]{1,0:T(8,128)(2,1)} %get-tuple-element.88), channel_id=1, source_target_pairs={{0,1},{1,0},{2,3},{3,2},{4,5},{5,4},{6,7},{7,6},{8,9},{9,8},{10,11... | collective-permute-start | bytes 2359304 | tf_op jit(solution)/shard_map/ppermute | solution.py:310
  332.1 24.4 %collective-permute-start.32 = (bf16[128,2048]{1,0:T(8,128)(2,1)}, bf16[128,2048]{1,0:T(8,128)(2,1)S(1)}, u32[]{:S(2)}, u32[]{:S(2)}) collective-permute-start(bf16[128,2048]{1,0:T(8,128)(2,1)} %copy-done.37), channel_id=1, source_target_pairs={{0,2},{2,4},{4,6},{6,8},{8,10},{10,12},{12,14},{14,16},{16,18},{18... | collective-permute-start | bytes 1572872 | tf_op jit(solution)/shard_map/ppermute | solution.py:307
  332.2 24.3 %collective-permute-start.57 = (bf16[128,2048]{1,0:T(8,128)(2,1)}, bf16[128,2048]{1,0:T(8,128)(2,1)S(1)}, u32[]{:S(2)}, u32[]{:S(2)}) collective-permute-start(bf16[128,2048]{1,0:T(8,128)(2,1)} %copy-done.38), channel_id=1, source_target_pairs={{0,62},{2,0},{4,2},{6,4},{8,6},{10,8},{12,10},{14,12},{16,14},{18,... | collective-permute-start | bytes 1572872 | tf_op jit(solution)/shard_map/ppermute | solution.py:307
  362.9 27.1 %collective-permute-start.75 = (bf16[96,4096]{1,0:T(8,128)(2,1)}, bf16[96,4096]{1,0:T(8,128)(2,1)S(1)}, u32[]{:S(2)}, u32[]{:S(2)}) collective-permute-start(bf16[96,4096]{1,0:T(8,128)(2,1)} %get-tuple-element.91), channel_id=1, source_target_pairs={{0,1},{1,0},{2,3},{3,2},{4,5},{5,4},{6,7},{7,6},{8,9},{9,8},{10,11... | collective-permute-start | bytes 2359304 | tf_op jit(solution)/shard_map/ppermute | solution.py:310
  365.7 24.4 %collective-permute-start.33 = (bf16[128,2048]{1,0:T(8,128)(2,1)}, bf16[128,2048]{1,0:T(8,128)(2,1)S(1)}, u32[]{:S(2)}, u32[]{:S(2)}) collective-permute-start(bf16[128,2048]{1,0:T(8,128)(2,1)} %copy-done.41), channel_id=1, source_target_pairs={{0,2},{2,4},{4,6},{6,8},{8,10},{10,12},{12,14},{14,16},{16,18},{18... | collective-permute-start | bytes 1572872 | tf_op jit(solution)/shard_map/ppermute | solution.py:307
  365.9 24.2 %collective-permute-start.58 = (bf16[128,2048]{1,0:T(8,128)(2,1)}, bf16[128,2048]{1,0:T(8,128)(2,1)S(1)}, u32[]{:S(2)}, u32[]{:S(2)}) collective-permute-start(bf16[128,2048]{1,0:T(8,128)(2,1)} %copy-done.42), channel_id=1, source_target_pairs={{0,62},{2,0},{4,2},{6,4},{8,6},{10,8},{12,10},{14,12},{16,14},{18,... | collective-permute-start | bytes 1572872 | tf_op jit(solution)/shard_map/ppermute | solution.py:307
  396.5 27.1 %collective-permute-start.76 = (bf16[96,4096]{1,0:T(8,128)(2,1)}, bf16[96,4096]{1,0:T(8,128)(2,1)S(1)}, u32[]{:S(2)}, u32[]{:S(2)}) collective-permute-start(bf16[96,4096]{1,0:T(8,128)(2,1)} %get-tuple-element.94), channel_id=1, source_target_pairs={{0,1},{1,0},{2,3},{3,2},{4,5},{5,4},{6,7},{7,6},{8,9},{9,8},{10,11... | collective-permute-start | bytes 2359304 | tf_op jit(solution)/shard_map/ppermute | solution.py:310
  399.2 24.4 %collective-permute-start.34 = (bf16[128,2048]{1,0:T(8,128)(2,1)}, bf16[128,2048]{1,0:T(8,128)(2,1)S(1)}, u32[]{:S(2)}, u32[]{:S(2)}) collective-permute-start(bf16[128,2048]{1,0:T(8,128)(2,1)} %copy-done.45), channel_id=1, source_target_pairs={{0,2},{2,4},{4,6},{6,8},{8,10},{10,12},{12,14},{14,16},{16,18},{18... | collective-permute-start | bytes 1572872 | tf_op jit(solution)/shard_map/ppermute | solution.py:307
  430.0 27.1 %collective-permute-start.77 = (bf16[96,4096]{1,0:T(8,128)(2,1)}, bf16[96,4096]{1,0:T(8,128)(2,1)S(1)}, u32[]{:S(2)}, u32[]{:S(2)}) collective-permute-start(bf16[96,4096]{1,0:T(8,128)(2,1)} %get-tuple-element.97), channel_id=1, source_target_pairs={{0,1},{1,0},{2,3},{3,2},{4,5},{5,4},{6,7},{7,6},{8,9},{9,8},{10,11... | collective-permute-start | bytes 2359304 | tf_op jit(solution)/shard_map/ppermute | solution.py:310
  432.8 24.4 %collective-permute-start.35 = (bf16[128,2048]{1,0:T(8,128)(2,1)}, bf16[128,2048]{1,0:T(8,128)(2,1)S(1)}, u32[]{:S(2)}, u32[]{:S(2)}) collective-permute-start(bf16[128,2048]{1,0:T(8,128)(2,1)} %copy-done.49), channel_id=1, source_target_pairs={{0,2},{2,4},{4,6},{6,8},{8,10},{10,12},{12,14},{14,16},{16,18},{18... | collective-permute-start | bytes 1572872 | tf_op jit(solution)/shard_map/ppermute | solution.py:307
  463.6 27.7 %collective-permute-start.78 = (bf16[96,4096]{1,0:T(8,128)(2,1)}, bf16[96,4096]{1,0:T(8,128)(2,1)S(1)}, u32[]{:S(2)}, u32[]{:S(2)}) collective-permute-start(bf16[96,4096]{1,0:T(8,128)(2,1)} %get-tuple-element.100), channel_id=1, source_target_pairs={{0,1},{1,0},{2,3},{3,2},{4,5},{5,4},{6,7},{7,6},{8,9},{9,8},{10,11... | collective-permute-start | bytes 2359304 | tf_op jit(solution)/shard_map/ppermute | solution.py:310
  466.4 24.8 %collective-permute-start.36 = (bf16[128,2048]{1,0:T(8,128)(2,1)}, bf16[128,2048]{1,0:T(8,128)(2,1)}, u32[]{:S(2)}, u32[]{:S(2)}) collective-permute-start(bf16[128,2048]{1,0:T(8,128)(2,1)} %copy-done.53), channel_id=1, source_target_pairs={{0,2},{2,4},{4,6},{6,8},{8,10},{10,12},{12,14},{14,16},{16,18},{18... | collective-permute-start | bytes 1572872 | tf_op jit(solution)/shard_map/ppermute | solution.py:307
  466.7 24.5 %collective-permute-start.61 = (bf16[128,2048]{1,0:T(8,128)(2,1)}, bf16[128,2048]{1,0:T(8,128)(2,1)}, u32[]{:S(2)}, u32[]{:S(2)}) collective-permute-start(bf16[128,2048]{1,0:T(8,128)(2,1)} %copy-done.54), channel_id=1, source_target_pairs={{0,62},{2,0},{4,2},{6,4},{8,6},{10,8},{12,10},{14,12},{16,14},{18,... | collective-permute-start | bytes 1572872 | tf_op jit(solution)/shard_map/ppermute | solution.py:307
  497.3 27.0 %collective-permute-start.79 = (bf16[96,4096]{1,0:T(8,128)(2,1)}, bf16[96,4096]{1,0:T(8,128)(2,1)S(1)}, u32[]{:S(2)}, u32[]{:S(2)}) collective-permute-start(bf16[96,4096]{1,0:T(8,128)(2,1)} %get-tuple-element.103), channel_id=1, source_target_pairs={{0,1},{1,0},{2,3},{3,2},{4,5},{5,4},{6,7},{7,6},{8,9},{9,8},{10,11... | collective-permute-start | bytes 2359304 | tf_op jit(solution)/shard_map/ppermute | solution.py:310
  499.9 24.4 %collective-permute-start.37 = (bf16[128,2048]{1,0:T(8,128)(2,1)}, bf16[128,2048]{1,0:T(8,128)(2,1)S(1)}, u32[]{:S(2)}, u32[]{:S(2)}) collective-permute-start(bf16[128,2048]{1,0:T(8,128)(2,1)} %collective-permute-done.36.refs_3_), channel_id=1, source_target_pairs={{0,2},{2,4},{4,6},{6,8},{8,10},{10,12},{12,14},{14,16},{16,18},{18... | collective-permute-start | bytes 1572872 | tf_op jit(solution)/shard_map/ppermute | solution.py:307
  500.0 24.3 %collective-permute-start.62 = (bf16[128,2048]{1,0:T(8,128)(2,1)}, bf16[128,2048]{1,0:T(8,128)(2,1)S(1)}, u32[]{:S(2)}, u32[]{:S(2)}) collective-permute-start(bf16[128,2048]{1,0:T(8,128)(2,1)} %collective-permute-done.61.refs_5_), channel_id=1, source_target_pairs={{0,62},{2,0},{4,2},{6,4},{8,6},{10,8},{12,10},{14,12},{16,14},{18,... | collective-permute-start | bytes 1572872 | tf_op jit(solution)/shard_map/ppermute | solution.py:307
  (122 other events, 1430.7 us)
